TPU v7x, 256 devices: a whole 4x4x8 slice. The times are simulated.
256 devices in a mesh: dp: 32 (over z_lo, x, y), tensor: 8 (over z_hi, core).
Axes of the slice: x: 4, y: 4, z: 8 (z_hi: 4, z_lo: 2; z = z_hi * 2 + z_lo), core: 2. Of those that a mesh axis runs over, the one named last changes fastest.
Arguments:
- hidden: bfloat16 [4096, 8192], P('dp')
- q_weight: float32 [8192, 4096], P(('dp', 'tensor')), may hold values from -0.0625 to 0.0625
- k_weight: float32 [8192, 1024], P(('dp', 'tensor')), may hold values from -0.0625 to 0.0625
- v_weight: float32 [8192, 1024], P(('dp', 'tensor')), may hold values from -0.0625 to 0.0625
- o_weight: float32 [8192, 4096], P(('dp', 'tensor')), may hold values from -0.09375 to 0.09375
- input_gain: float32 [8192], replicated, may hold values from 0.25 to 1.75
- post_gain: float32 [8192], replicated, may hold values from 0.25 to 1.75
- key_cache: bfloat16 [4096, 64, 8, 128], P('dp', None, 'tensor'), may hold values from -1000 to 1000
- value_cache: bfloat16 [4096, 64, 8, 128], P('dp', None, 'tensor'), may hold values from -6 to 6
- lengths: int32 [4096], P('dp'), may hold values from 1 to 64
Outputs:
- new_hidden: bfloat16 [4096, 8192], P('dp')
- normed: bfloat16 [4096, 8192], P('dp')
- fresh_token_keys: bfloat16 [4096, 8, 128], P('dp', 'tensor')
- new_values: bfloat16 [4096, 8, 128], P('dp', 'tensor')
All inputs are finite; a program needn't handle non-finite values.
Results may differ from a plain program's by a relative error of at most 0.012.
The roundings to bfloat16 on the way count: a program that leaves them out, or rounds other values in their place, can miss the bound.
Values may be sent and summed in bfloat16 or wider, within the bound.
A program may use at most 128 MiB of HBM per device.

v0:
```python
import math

import jax
import jax.numpy as jnp
from jax import lax
from jax.sharding import PartitionSpec as P

HEADS = 32
KV_HEADS = 8
HEAD_DIM = 128


epsilon = 1e-05
rope_base = 500000.0


def side_by_side(arrays, axis, dim, along):
    ends, at = ([], 0)
    for a in arrays[:-1]:
        at += a.shape[along]
        ends.append(at)
    both = jnp.concatenate(arrays, axis=along)
    return tuple(jnp.split(lax.all_gather(both, axis, axis=dim, tiled=True), ends, axis=along))


def rms_gain(values, gain_vector):
    mean_square = jnp.mean(values * values, axis=-1, keepdims=True)
    return values * lax.rsqrt(mean_square + epsilon) * gain_vector


def rotate(values, positions):
    half_dim = values.shape[-1] // 2
    index_row = jnp.arange(half_dim, dtype=jnp.float32)
    frequency = jnp.exp(-math.log(rope_base) * index_row / half_dim)
    angle = positions.astype(jnp.float32)[:, None, None] * frequency[None, None, :]
    first_half = values[..., :half_dim]
    second_half = values[..., half_dim:]
    return jnp.concatenate(
        [
            first_half * jnp.cos(angle) - second_half * jnp.sin(angle),
            second_half * jnp.cos(angle) + first_half * jnp.sin(angle),
        ],
        axis=-1,
    )


def attend(query_b, fresh_token_keys, new_values, key_cache, value_cache, lengths):
    row_count, kv_count = (fresh_token_keys.shape[0], fresh_token_keys.shape[1])
    grouped_heads = query_b.reshape(row_count, kv_count, -1, HEAD_DIM)
    reciprocal_root = 1.0 / math.sqrt(HEAD_DIM)
    scores = (
        jnp.einsum("bkgd,blkd->bkgl", grouped_heads, key_cache, preferred_element_type=jnp.float32)
        * reciprocal_root
    )
    self_token_score = (
        jnp.einsum(
            "lfxa,lfa->lfx", grouped_heads, fresh_token_keys, preferred_element_type=jnp.float32
        )
        * reciprocal_root
    )
    visible = jnp.arange(key_cache.shape[1], dtype=jnp.int32)[None, :] < lengths[:, None]
    scores = jnp.where(visible[:, None, None, :], scores, -jnp.inf)
    largest = jnp.maximum(jnp.max(scores, axis=-1), self_token_score)
    kept_exp = jnp.exp(scores - largest[..., None])
    own_exp = jnp.exp(self_token_score - largest)
    softmax_divisor = jnp.sum(kept_exp, axis=-1) + own_exp
    weights_kept = (kept_exp / softmax_divisor[..., None]).astype(jnp.bfloat16)
    own_weight = (own_exp / softmax_divisor).astype(jnp.bfloat16)
    attended = jnp.einsum(
        "bkgl,blkd->bkgd", weights_kept, value_cache, preferred_element_type=jnp.float32
    )
    attended = (
        attended
        + own_weight.astype(jnp.float32)[..., None] * new_values.astype(jnp.float32)[:, :, None, :]
    )
    return attended.reshape(row_count, -1).astype(jnp.bfloat16)


def shards(
    hidden,
    q_weight,
    k_weight,
    v_weight,
    o_weight,
    input_gain,
    post_gain,
    key_cache,
    value_cache,
    lengths,
):
    tensor_size = lax.axis_size("tensor")
    row_count = hidden.shape[0]
    heads_here = HEADS // tensor_size
    kv_here = KV_HEADS // tensor_size
    w_query, w_key, value_matrix, w_out = (
        lax.all_to_all(
            q_weight.astype(jnp.bfloat16), "tensor", split_axis=1, concat_axis=0, tiled=True
        ),
        lax.all_to_all(
            k_weight.astype(jnp.bfloat16), "tensor", split_axis=1, concat_axis=0, tiled=True
        ),
        lax.all_to_all(
            v_weight.astype(jnp.bfloat16), "tensor", split_axis=1, concat_axis=0, tiled=True
        ),
        lax.all_to_all(
            o_weight.astype(jnp.bfloat16), "tensor", split_axis=1, concat_axis=0, tiled=True
        ),
    )
    normal_in = rms_gain(hidden.astype(jnp.float32), input_gain).astype(jnp.bfloat16)
    portions = side_by_side((w_query, w_key, value_matrix), "dp", 0, 1)
    query, key_part, value_part = tuple(
        (jnp.dot(normal_in, portion, preferred_element_type=jnp.float32) for portion in portions)
    )
    query_b = rotate(query.reshape(row_count, heads_here, HEAD_DIM), lengths).astype(jnp.bfloat16)
    fresh_token_keys = rotate(key_part.reshape(row_count, kv_here, HEAD_DIM), lengths).astype(
        jnp.bfloat16
    )
    new_values = value_part.reshape(row_count, kv_here, HEAD_DIM).astype(jnp.bfloat16)
    attended = attend(query_b, fresh_token_keys, new_values, key_cache, value_cache, lengths)
    partial_value = lax.dot_general(
        attended,
        lax.all_gather(w_out, "dp", axis=0, tiled=True),
        (((1,), (1,)), ((), ())),
        preferred_element_type=jnp.float32,
    )
    mixed = lax.psum(partial_value.astype(jnp.bfloat16), "tensor").astype(jnp.float32)
    residual = hidden.astype(jnp.float32) + mixed
    new_hidden = residual.astype(jnp.bfloat16)
    normed = rms_gain(residual, post_gain).astype(jnp.bfloat16)
    return (new_hidden, normed, fresh_token_keys, new_values)


def solution(mesh):
    in_specs = (
        P("dp", None),
        P(("dp", "tensor"), None),
        P(("dp", "tensor"), None),
        P(("dp", "tensor"), None),
        P(("dp", "tensor"), None),
        P(),
        P(),
        P("dp", None, "tensor", None),
        P("dp", None, "tensor", None),
        P("dp"),
    )
    out_specs = (P("dp", None), P("dp", None), P("dp", "tensor", None), P("dp", "tensor", None))
    return jax.shard_map(shards, mesh=mesh, in_specs=in_specs, out_specs=out_specs, check_vma=False)
```

profile of v0, /device:TPU:1, one launch (start us, length us, event | category | flops | bytes accessed | tf_op | source)
XLA Modules:
  0.0 503.5 jit_solution(8640591926322045796)
XLA Ops:
  7.2 0.0 copy-start
  7.2 0.0 copy-start.4
  7.2 0.0 copy-start.5
  7.2 1.7 copy_bitcast_fusion.3
  8.9 10.0 %all-to-all-start.1 = ((bf16[32,8,128]{2,0,1:T(8,128)(2,1)}), bf16[32,8,128]{2,0,1:T(8,128)(2,1)S(1)}, u32[]{:S(2)}, u32[]{:S(2)}) async-start(bf16[32,8,128]{2,0,1:T(8,128)(2,1)} %copy_bitcast_fusion.3), calls=%async_computation.1 | async-start | bytes 131072 | tf_op jit(solution)/shard_map/all_to_all | solution.py:99
  18.8 1.5 copy_bitcast_fusion.2
  20.4 6.0 %all-to-all-done.1 = bf16[32,8,128]{2,0,1:T(8,128)(2,1)S(1)} async-done(((bf16[32,8,128]{2,0,1:T(8,128)(2,1)}), bf16[32,8,128]{2,0,1:T(8,128)(2,1)S(1)}, u32[]{:S(2)}, u32[]{:S(2)}) %all-to-all-start.1) | async-done | bytes 65568 | tf_op jit(solution)/shard_map/all_to_all | solution.py:99
  26.4 4.0 all-to-all-start.2
  30.4 0.0 all-gather.3.cloned.1.call-start
  30.4 1.1 convert_element_type.79
  31.5 6.5 %all-to-all-done.2 = bf16[32,8,128]{2,0,1:T(8,128)(2,1)S(1)} async-done(((bf16[32,8,128]{2,0,1:T(8,128)(2,1)}), bf16[32,8,128]{2,0,1:T(8,128)(2,1)S(1)}, u32[]{:S(2)}, u32[]{:S(2)}) %all-to-all-start.2) | async-done | bytes 65568 | tf_op jit(solution)/shard_map/all_to_all | solution.py:102
  38.0 12.5 %all_to_all.76 = bf16[32,8,512]{2,0,1:T(8,128)(2,1)S(1)} all-to-all(bf16[32,8,512]{2,0,1:T(8,128)(2,1)S(1)} %bitcast.62), channel_id=1, replica_groups=mesh['dp'=32,'tensor'=8] {'tensor'}, dimensions={1} | all-to-all | bytes 524288 | tf_op jit(solution)/shard_map/all_to_all | solution.py:96
  50.5 0.8 pad_maximum_fusion
  51.3 0.0 all-gather.3.cloned.1.call-update
  51.3 0.0 all-gather.5.cloned.1.call-start
  51.4 1.1 convert_element_type.90
  52.5 17.4 %all_to_all.77 = bf16[32,8,512]{2,0,1:T(8,128)(2,1)} all-to-all(bf16[32,8,512]{2,0,1:T(8,128)(2,1)S(1)} %bitcast.63), channel_id=1, replica_groups=mesh['dp'=32,'tensor'=8] {'tensor'}, dimensions={1} | all-to-all | bytes 524288 | tf_op jit(solution)/shard_map/all_to_all | solution.py:105
  69.8 0.0 all-gather.5.cloned.1.call-update
  69.8 0.0 all-reduce.2.cloned.1.call-start
  69.9 0.0 copy-done.4
  69.9 2.1 fusion.2
  72.0 0.1 iota_compare_fusion
  72.1 0.3 multiply_cosine_fusion
  72.4 139.6 %all-gather.3.cloned.1.call-done = bf16[8192,768]{1,0:T(8,128)(2,1)} async-done(((bf16[256,768]{1,0:T(8,128)(2,1)}), bf16[8192,768]{1,0:T(8,128)(2,1)}) %all-gather.3.cloned.1.call-update) | async-done | bytes 12582928 | tf_op jit(solution)/shard_map/all_gather | solution.py:23
  212.0 0.0 copy-done.5
  212.0 3.3 fusion.26
  215.3 0.2 fusion.42
  215.5 0.1 copy.49
  215.6 5.3 %fusion = f32[128,512]{1,0:T(8,128)S(1)} fusion(bf16[8192,768]{1,0:T(8,128)(2,1)} %all-gather.3.cloned.1.call-done, bf16[128,8192]{1,0:T(8,128)(2,1)} %param.10, f32[8192]{0:T(1024)S(1)} %copy-done.5, f32[128]{0:T(128)S(1)} %add_rsqrt_fusion.1), kind=kOutput, calls=%fused_computation.1 | convolution fusion | flops 1077936128 | bytes 10781184 | tf_op jit(solution)/shard_map/dot_general | solution.py:112
  221.0 0.1 reshape.271
  221.1 0.3 subtract_convert_fusion
  221.4 0.3 multiply_reduce_fusion.1
  221.7 0.1 copy.48
  221.8 2.9 fusion.51
  224.7 0.1 copy.37
  224.8 0.1 copy.38
  224.9 0.4 fusion.32
  225.3 0.1 copy.39
  225.4 0.1 copy.40
  225.5 0.1 copy.41
  225.6 3.7 fusion.50
  229.3 0.0 copy-done
  229.3 0.7 fusion.23
  230.0 147.6 %all-gather.5.cloned.1.call-done = bf16[8192,512]{1,0:T(8,128)(2,1)} async-done(((bf16[256,512]{1,0:T(8,128)(2,1)}), bf16[8192,512]{1,0:T(8,128)(2,1)}) %all-gather.5.cloned.1.call-update) | async-done | bytes 8388624 | tf_op jit(solution)/shard_map/all_gather | solution.py:122
  377.7 7.5 %convolution_convert_fusion = bf16[128,8192]{1,0:T(8,128)(2,1)} fusion(bf16[8192,512]{1,0:T(8,128)(2,1)} %all-gather.5.cloned.1.call-done, bf16[16,8,4,128]{3,2,1,0:T(4,128)(2,1)S(1)} %bitcast.68), kind=kOutput, calls=%fused_computation | convolution fusion | flops 1074790400 | bytes 10616832 | tf_op jit(solution)/shard_map/dot_general | solution.py:120
  385.2 0.0 copy-start.3
  385.2 0.0 all-reduce.2.cloned.1.call-update
  385.2 0.7 copy.43
  386.0 104.3 %all-reduce.2.cloned.1.call-done = bf16[128,8192]{1,0:T(8,128)(2,1)} async-done(((bf16[128,8192]{1,0:T(8,128)(2,1)}), bf16[128,8192]{1,0:T(8,128)(2,1)}) %all-reduce.2.cloned.1.call-update) | async-done | bytes 2097168 | tf_op jit(solution)/shard_map/psum | solution.py:126
  490.3 0.0 copy-start.1
  490.3 0.0 copy-start.2
  490.3 3.1 multiply_reduce_fusion
  493.4 0.0 copy-done.3
  493.4 0.0 copy-done.1
  493.4 0.3 copy-done.2
  493.8 3.2 multiply_convert_fusion
  (10 shorter events, 0.1 us)
Async XLA Ops:
  7.2 222.1 %copy-start = (bf16[128,64,1,128]{3,1,2,0:T(8,128)(2,1)S(1)}, bf16[128,64,1,128]{3,1,2,0:T(8,128)(2,1)}, u32[]{:S(2)}) copy-start(bf16[128,64,1,128]{3,1,2,0:T(8,128)(2,1)} %param.18) | copy-start | bytes 6291460
  7.2 62.7 %copy-start.4 = (s32[128]{0:T(128)S(1)}, s32[128]{0:T(128)}, u32[]{:S(2)}) copy-start(s32[128]{0:T(128)} %param.19) | copy-start | bytes 1540
  7.2 204.8 %copy-start.5 = (f32[8192]{0:T(1024)S(1)}, f32[8192]{0:T(1024)}, u32[]{:S(2)}) copy-start(f32[8192]{0:T(1024)} %param.15) | copy-start | bytes 98308
  8.9 17.5 %all-to-all-start.1 = ((bf16[32,8,128]{2,0,1:T(8,128)(2,1)}), bf16[32,8,128]{2,0,1:T(8,128)(2,1)S(1)}, u32[]{:S(2)}, u32[]{:S(2)}) async-start(bf16[32,8,128]{2,0,1:T(8,128)(2,1)} %copy_bitcast_fusion.3), calls=%async_computation.1 | async-start | bytes 131072 | tf_op jit(solution)/shard_map/all_to_all | solution.py:99
  26.4 11.6 %all-to-all-start.2 = ((bf16[32,8,128]{2,0,1:T(8,128)(2,1)}), bf16[32,8,128]{2,0,1:T(8,128)(2,1)S(1)}, u32[]{:S(2)}, u32[]{:S(2)}) async-start(bf16[32,8,128]{2,0,1:T(8,128)(2,1)} %copy_bitcast_fusion.2), calls=%async_computation.2 | async-start | bytes 131072 | tf_op jit(solution)/shard_map/all_to_all | solution.py:102
  30.4 181.6 %all-gather.3.cloned.1.call-start = ((), (), s32[]{:S(2)}) async-start(), calls=%async_computation.4 | async-start | bytes 12976128 | tf_op jit(solution)/shard_map/all_gather | solution.py:23
  51.3 326.4 %all-gather.5.cloned.1.call-start = ((), (), s32[]{:S(2)}) async-start(), calls=%async_computation.5 | async-start | bytes 8650752 | tf_op jit(solution)/shard_map/all_gather | solution.py:122
  69.8 420.4 %all-reduce.2.cloned.1.call-start = ((), (), s32[]{:S(2)}) async-start(), calls=%async_computation.6 | async-start | bytes 4194304 | tf_op jit(solution)/shard_map/psum | solution.py:126
  385.2 108.2 %copy-start.3 = (f32[8192]{0:T(1024)S(1)}, f32[8192]{0:T(1024)}, u32[]{:S(2)}) copy-start(f32[8192]{0:T(1024)} %param.16) | copy-start | bytes 98308
  490.3 3.2 copy-start.1
  490.3 3.5 copy-start.2
Sparse Core Ops, SparseCore 0:
  51.4 160.5 all-gather.2
  213.8 163.8 all-gather.4
  385.3 104.8 all-reduce.1
where the time goes:
time: 505 us; the launch traced here: 504 us
  waiting for transfers between devices  404 us (80%)
  blocking collectives  29.9 us (6%)
  matrix products  23.5 us (5%)
  other arithmetic  16.3 us (3%)
  starting transfers between devices  14.1 us (3%)
  between operations  13.9 us (3%)
    all_gather x1, waiting for transfers between devices, shards(): lax.all_gather(w_out, 'dp', axis=0, tiled=True)  148 us
    all_gather x1, waiting for transfers between devices, side_by_side(): lax.all_gather(both, axis, axis=dim, tiled=True)  140 us
    psum x1, waiting for transfers between devices, shards(): lax.psum(partial_value.astype(jnp.bfloat16), 'tensor').astype(jnp.float32)  104 us
    all_to_all x1, blocking collectives, shards(): lax.all_to_all(o_weight.astype(jnp.bfloat16), 'tensor', split_axis=1, con...  17.4 us
    all_to_all x1, blocking collectives, shards(): lax.all_to_all(q_weight.astype(jnp.bfloat16), 'tensor', split_axis=1, con...  12.5 us
    dot_general x3, matrix products, shards(): jnp.dot(normal_in, portion, preferred_element_type=jnp.float32)  12.3 us
  transfers between devices with their start and end apart: 5, of which 5 were waited for; matrix products, arithmetic and copies ran while one was open for 5% of the time, Pallas kernels for 0%

commit v1 on v0

v1 whole, which is shorter than its diff:
```python
import math

import jax
import jax.numpy as jnp
from jax import lax
from jax.experimental import pallas as pl
from jax.experimental.pallas import tpu as pltpu
from jax.sharding import PartitionSpec as P

HEAD_DIM = 128
GROUP = 4
ROWS = 128
D = 8192
CACHE = 64
QC = GROUP * HEAD_DIM
WC = QC + 2 * HEAD_DIM
K = 1024
BLOCK_ROWS = 8

epsilon = 1e-05
rope_base = 500000.0

PEERS = [(1, 0), (1, 1), (1, 3), (1, 2), (0, 1), (0, 3), (0, 2)]


def remote(src, dst, send, recv, dp, tensor):
    return pltpu.make_async_remote_copy(
        src_ref=src,
        dst_ref=dst,
        send_sem=send,
        recv_sem=recv,
        device_id={"dp": dp, "tensor": tensor},
        device_id_type=pl.DeviceIdType.MESH,
    )


def kernel(
    hidden_in,
    qw_in,
    kw_in,
    vw_in,
    ow_in,
    gain_in,
    post_in,
    kc_in,
    vc_in,
    cos_in,
    sin_in,
    len_in,
    new_out,
    normed_out,
    fresh_out,
    value_out,
    hidden,
    qw,
    kw,
    vw,
    ow,
    gain,
    post,
    kc,
    vc,
    cos,
    sin,
    lens,
    xn,
    wst,
    ost,
    wg,
    og,
    a,
    pst,
    crecv,
    own,
    probs,
    att32,
    attg,
    half,
    hrecv,
    summed,
    sst,
    srecv,
    tst,
    g,
    gall,
    residual,
    new_v,
    normed_v,
    fresh_v,
    value_v,
    in_sem,
    out_sem,
    b1_s,
    b1_r,
    b2_s,
    b2_r,
    o1_s,
    o1_r,
    o2_s,
    o2_r,
    a_s,
    a_r,
    af_s,
    af_r,
    c_s,
    c_r,
    g_s,
    g_r,
    h_s,
    h_r,
    s_s,
    s_r,
    t_s,
    t_r,
    u_s,
    u_r,
    uf_s,
    uf_r,
):
    dp = lax.axis_index("dp")
    t = lax.axis_index("tensor")
    y = dp % 4
    x = (dp // 4) % 4
    zl = dp // 16
    k = dp // 4
    zh = t // 2
    c = t % 2
    mate = t + 1 - 2 * c

    def member(dz, i):
        return ((zl + dz) % 2) * 4 + (x + i) % 4

    def source(dz, i):
        return ((zl + dz) % 2) * 4 + (x - i + 4) % 4

    def shifted(dz):
        if dz == 0:
            return t
        return ((zh - c * (1 - 2 * zl) + 4) % 4) * 2 + c

    loads = [
        pltpu.make_async_copy(src, dst, in_sem.at[n])
        for n, (src, dst) in enumerate(
            (
                (qw_in, qw),
                (kw_in, kw),
                (vw_in, vw),
                (hidden_in, hidden),
                (gain_in, gain),
                (ow_in, ow),
                (cos_in, cos),
                (sin_in, sin),
                (len_in, lens),
                (kc_in, kc),
                (vc_in, vc),
                (post_in, post),
            )
        )
    ]
    for copy in loads:
        copy.start()

    barrier = pltpu.get_barrier_semaphore()
    greeted = [(member(dz, i) * 4 + y, t) for dz, i in PEERS]
    greeted += [(member(1, i) * 4 + y, shifted(1)) for i in range(4)]
    greeted += [(dp, (t + j) % 8) for j in range(1, 8)]
    greeted += [(k * 4 + (y + i) % 4, t) for i in range(1, 4)]
    for peer in greeted:
        pl.semaphore_signal(
            barrier,
            inc=1,
            device_id={"dp": peer[0], "tensor": peer[1]},
            device_id_type=pl.DeviceIdType.MESH,
        )

    sent = []

    for n in (0, 1, 2):
        loads[n].wait()
    for j in range(8):
        wst[j, :, :QC] = qw[:, j * QC : (j + 1) * QC].astype(jnp.bfloat16)
        wst[j, :, QC : QC + HEAD_DIM] = kw[:, j * HEAD_DIM : (j + 1) * HEAD_DIM].astype(
            jnp.bfloat16
        )
        wst[j, :, QC + HEAD_DIM :] = vw[:, j * HEAD_DIM : (j + 1) * HEAD_DIM].astype(jnp.bfloat16)
    wg[y, t] = wst[t]
    pl.semaphore_wait(barrier, len(greeted))

    order = [4, 2, 6, 3, 5, 1, 7]
    b1 = {}
    for j in order:
        to = (t + j) % 8
        b1[j] = remote(wst.at[to], wg.at[y, t], b1_s.at[j], b1_r.at[j], dp, to)
        b1[j].start()
    sent += b1.values()

    loads[3].wait()
    loads[4].wait()

    def norm_rows(n, carry):
        rows = pl.ds(pl.multiple_of(n * 16, 16), 16)
        values = hidden[rows, :].astype(jnp.float32)
        mean_square = jnp.mean(values * values, axis=-1, keepdims=True)
        normal = (values * lax.rsqrt(mean_square + epsilon) * gain[...]).astype(jnp.bfloat16)
        for m in range(8):
            xn[m, rows, :] = normal[:, m * K : (m + 1) * K]
        return carry

    lax.fori_loop(0, ROWS // 16, norm_rows, 0)

    mine = pl.ds(pl.multiple_of(c * 64, 64), 64)
    ac = {}
    for dz, i in PEERS:
        to = member(dz, i)
        ac[dz, i] = remote(
            xn.at[to, mine],
            a.at[k, mine],
            a_s.at[dz, i],
            a_r.at[dz, i],
            to * 4 + y,
            shifted(dz),
        )
        ac[dz, i].start()
    sent += ac.values()
    a[k] = xn[k]

    loads[5].wait()
    for j in range(8):
        ost[j] = ow[:, j * QC : (j + 1) * QC].astype(jnp.bfloat16)
    og[y, t] = ost[t]
    o1 = {}
    for j in order:
        to = (t + j) % 8
        o1[j] = remote(ost.at[to], og.at[y, t], o1_s.at[j], o1_r.at[j], dp, to)
        o1[j].start()
    sent += o1.values()

    b2 = {}
    for j in [0, 1, 7, 2, 6, 3, 5, 4]:
        if j:
            b1[j].wait_recv()
        origin = (t - j + 8) % 8
        for i in (1, 3, 2):
            b2[j, i] = remote(
                wg.at[y, origin],
                wg.at[y, origin],
                b2_s.at[j, i],
                b2_r.at[j, i],
                k * 4 + (y + i) % 4,
                t,
            )
            b2[j, i].start()
    sent += b2.values()

    af = {}
    for dz, i in [(1, 0), (0, 1), (0, 3), (1, 1), (1, 3), (0, 2), (1, 2)]:
        ac[dz, i].wait_recv()
        at = a.at[source(dz, i), mine]
        af[dz, i] = remote(at, at, af_s.at[dz, i], af_r.at[dz, i], dp, mate)
        af[dz, i].start()
    sent += af.values()

    for copy in b2.values():
        copy.wait_recv()
    for copy in af.values():
        copy.wait_recv()

    weights = wg[...].reshape(K, WC)
    cc = {}
    for dz in (1, 0):
        part = (zl + dz) % 2
        rows = a[pl.ds(part * 4, 4)].reshape(4 * ROWS, K)
        out = jnp.dot(rows, weights, preferred_element_type=jnp.float32).reshape(4, ROWS, WC)
        pst[pl.ds(part * 4, 4)] = out.astype(jnp.bfloat16)
        for i in (1, 3, 2, 0):
            if (dz, i) == (0, 0):
                continue
            to = member(dz, i)
            cc[dz, i] = remote(
                pst.at[to], crecv.at[dz, i], c_s.at[dz, i], c_r.at[dz, i], to * 4 + y, t
            )
            cc[dz, i].start()
    sent += cc.values()

    o2 = {}
    for j in [0, 1, 7, 2, 6, 3, 5, 4]:
        if j:
            o1[j].wait_recv()
        origin = (t - j + 8) % 8
        for i in (1, 3, 2):
            o2[j, i] = remote(
                og.at[y, origin],
                og.at[y, origin],
                o2_s.at[j, i],
                o2_r.at[j, i],
                k * 4 + (y + i) % 4,
                t,
            )
            o2[j, i].start()
    sent += o2.values()

    own[...] = pst[k].astype(jnp.float32)
    for dz, i in [(1, 0), (0, 1), (0, 3), (1, 1), (1, 3), (0, 2), (1, 2)]:
        cc[dz, i].wait_recv()
        own[...] += crecv[dz, i].astype(jnp.float32)

    for n in range(6, 11):
        loads[n].wait()

    cosine = cos[...]
    sine = sin[...]
    for h in range(GROUP + 1):
        columns = slice(h * HEAD_DIM, (h + 1) * HEAD_DIM)
        head = own[:, columns]
        head = head * cosine + pltpu.roll(head, 64, 1) * sine
        own[:, columns] = head.astype(jnp.bfloat16).astype(jnp.float32)
    fresh_v[...] = own[:, QC : QC + HEAD_DIM].astype(jnp.bfloat16)
    value_b = own[:, QC + HEAD_DIM :].astype(jnp.bfloat16)
    value_v[...] = value_b
    own[:, QC + HEAD_DIM :] = value_b.astype(jnp.float32)

    scale = 1.0 / math.sqrt(HEAD_DIM)
    wide = BLOCK_ROWS * CACHE
    tall = BLOCK_ROWS * GROUP
    row_of = lax.broadcasted_iota(jnp.int32, (tall, wide), 0) % BLOCK_ROWS
    column = lax.broadcasted_iota(jnp.int32, (tall, wide), 1)
    same = row_of == column // CACHE
    position = column % CACHE
    for n in range(ROWS // BLOCK_ROWS):
        rows = slice(n * BLOCK_ROWS, (n + 1) * BLOCK_ROWS)
        query = jnp.concatenate(
            [own[rows, h * HEAD_DIM : (h + 1) * HEAD_DIM] for h in range(GROUP)], axis=0
        )
        fresh = jnp.concatenate([own[rows, QC : QC + HEAD_DIM]] * GROUP, axis=0)
        length = jnp.concatenate([lens[rows, :]] * GROUP, axis=0)
        scores = (
            lax.dot_general(
                query.astype(jnp.bfloat16),
                kc[n * wide : (n + 1) * wide, :],
                (((1,), (1,)), ((), ())),
                preferred_element_type=jnp.float32,
            )
            * scale
        )
        self_score = jnp.sum(query * fresh, axis=-1, keepdims=True) * scale
        kept = same & (position < length)
        scores = jnp.where(kept, scores, -jnp.inf)
        largest = jnp.maximum(jnp.max(scores, axis=-1, keepdims=True), self_score)
        kept_exp = jnp.exp(scores - largest)
        own_exp = jnp.exp(self_score - largest)
        divisor = jnp.sum(kept_exp, axis=-1, keepdims=True) + own_exp
        probs[n] = (kept_exp / divisor).astype(jnp.bfloat16)
        own_prob = (own_exp / divisor).astype(jnp.bfloat16).astype(jnp.float32)
        value = jnp.concatenate([own[rows, QC + HEAD_DIM :]] * GROUP, axis=0)
        attended = (
            jnp.dot(
                probs[n],
                vc[n * wide : (n + 1) * wide, :],
                preferred_element_type=jnp.float32,
            )
            + own_prob * value
        )
        for h in range(GROUP):
            att32[rows, h * HEAD_DIM : (h + 1) * HEAD_DIM] = attended[
                h * BLOCK_ROWS : (h + 1) * BLOCK_ROWS
            ]

    attg[k] = att32[...].astype(jnp.bfloat16)
    gc = {}
    for dz, i in PEERS:
        gc[dz, i] = remote(
            attg.at[k], attg.at[k], g_s.at[dz, i], g_r.at[dz, i], member(dz, i) * 4 + y, t
        )
        gc[dz, i].start()
    sent += gc.values()

    for copy in o2.values():
        copy.wait_recv()
    for copy in gc.values():
        copy.wait_recv()

    hc = {}
    theirs_w = og[pl.ds((1 - c) * 2, 2)].reshape(512, QC)
    mine_w = og[pl.ds(c * 2, 2)].reshape(512, QC)
    for n in range(2):
        rows = attg[4 * n : 4 * n + 4].reshape(4 * ROWS, QC)
        half[n] = lax.dot_general(
            rows, theirs_w, (((1,), (1,)), ((), ())), preferred_element_type=jnp.float32
        ).astype(jnp.bfloat16)
        hc[n] = remote(half.at[n], hrecv.at[n], h_s.at[n], h_r.at[n], dp, mate)
        hc[n].start()
    sent += hc.values()
    for n in range(2):
        rows = attg[4 * n : 4 * n + 4].reshape(4 * ROWS, QC)
        summed[n] = lax.dot_general(
            rows, mine_w, (((1,), (1,)), ((), ())), preferred_element_type=jnp.float32
        )
    for n in range(2):
        hc[n].wait_recv()
        both = summed[n] + hrecv[n].astype(jnp.float32)
        for b in range(4):
            sst[b, n * 512 : (n + 1) * 512, :] = both[:, b * 128 : (b + 1) * 128].astype(
                jnp.bfloat16
            )
    sc = {}
    for j in (2, 1, 3):
        to = (zh + j) % 4
        sc[j] = remote(sst.at[to], srecv.at[j], s_s.at[j], s_r.at[j], dp, to * 2 + c)
        sc[j].start()
    sent += sc.values()
    for j in (1, 3, 2):
        sc[j].wait_recv()
    total = (
        sst[zh].astype(jnp.float32)
        + srecv[1].astype(jnp.float32)
        + srecv[2].astype(jnp.float32)
        + srecv[3].astype(jnp.float32)
    )
    tst[...] = total.astype(jnp.bfloat16).reshape(8, ROWS, 128)

    tc = {}
    for dz, i in PEERS:
        to = member(dz, i)
        tc[dz, i] = remote(
            tst.at[to], g.at[k], t_s.at[dz, i], t_r.at[dz, i], to * 4 + y, t
        )
        tc[dz, i].start()
    sent += tc.values()
    g[k] = tst[k]
    for copy in tc.values():
        copy.wait_recv()
    uc = {}
    for j in (2, 1, 3):
        to = (zh + j) % 4
        uc[j] = remote(g, gall.at[zh, c], u_s.at[j], u_r.at[j], dp, to * 2 + c)
        uc[j].start()
    uf = {}
    uf[0] = remote(g, gall.at[zh, c], uf_s.at[0], uf_r.at[0], dp, mate)
    uf[0].start()
    gall[zh, c] = g[...]
    for j in (1, 3, 2):
        uc[j].wait_recv()
        at = gall.at[(zh - j + 4) % 4, c]
        uf[j] = remote(at, at, uf_s.at[j], uf_r.at[j], dp, mate)
        uf[j].start()
    sent += uc.values()
    sent += uf.values()
    for copy in uf.values():
        copy.wait_recv()
    loads[11].wait()

    def finish(n, carry):
        rows = pl.ds(pl.multiple_of(n * 16, 16), 16)
        squares = jnp.zeros((16, 128), jnp.float32)
        for b in range(64):
            columns = slice(b * 128, (b + 1) * 128)
            mixed = gall[b % 4, (b // 4) % 2, b // 8, rows, :].astype(jnp.float32)
            value = hidden[rows, columns].astype(jnp.float32) + mixed
            new_v[rows, columns] = value.astype(jnp.bfloat16)
            residual[:, columns] = value
            squares += value * value
        mean_square = jnp.sum(squares, axis=-1, keepdims=True) * (1.0 / D)
        factor = lax.rsqrt(mean_square + epsilon)
        normed_v[rows, :] = (residual[...] * factor * post[...]).astype(jnp.bfloat16)
        return carry

    lax.fori_loop(0, ROWS // 16, finish, 0)

    stores = [
        pltpu.make_async_copy(src, dst, out_sem.at[n])
        for n, (src, dst) in enumerate(
            ((new_v, new_out), (normed_v, normed_out), (fresh_v, fresh_out), (value_v, value_out))
        )
    ]
    for copy in stores:
        copy.start()
    for copy in stores:
        copy.wait()
    for copy in sent:
        copy.wait_send()


def shards(
    hidden,
    q_weight,
    k_weight,
    v_weight,
    o_weight,
    input_gain,
    post_gain,
    key_cache,
    value_cache,
    lengths,
):
    half_dim = HEAD_DIM // 2
    index_row = jnp.arange(half_dim, dtype=jnp.float32)
    frequency = jnp.exp(-math.log(rope_base) * index_row / half_dim)
    angle = lengths.astype(jnp.float32)[:, None] * frequency[None, :]
    cosine, sine = jnp.cos(angle), jnp.sin(angle)
    cos = jnp.concatenate([cosine, cosine], axis=-1)
    sin = jnp.concatenate([-sine, sine], axis=-1)
    lens = lengths.astype(jnp.int32)[:, None]
    kc = jnp.transpose(key_cache, (0, 2, 1, 3)).reshape(ROWS * CACHE, HEAD_DIM)
    vc = jnp.transpose(value_cache, (0, 2, 1, 3)).reshape(ROWS * CACHE, HEAD_DIM)
    bf16, f32 = jnp.bfloat16, jnp.float32
    dma = pltpu.SemaphoreType.DMA
    new_hidden, normed, fresh, values = pl.pallas_call(
        kernel,
        out_shape=(
            jax.ShapeDtypeStruct((ROWS, D), bf16),
            jax.ShapeDtypeStruct((ROWS, D), bf16),
            jax.ShapeDtypeStruct((ROWS, HEAD_DIM), bf16),
            jax.ShapeDtypeStruct((ROWS, HEAD_DIM), bf16),
        ),
        in_specs=[pl.BlockSpec(memory_space=pl.ANY)] * 12,
        out_specs=[pl.BlockSpec(memory_space=pl.ANY)] * 4,
        scratch_shapes=[
            pltpu.VMEM((ROWS, D), bf16),
            pltpu.VMEM((32, 4096), f32),
            pltpu.VMEM((32, 1024), f32),
            pltpu.VMEM((32, 1024), f32),
            pltpu.VMEM((32, 4096), f32),
            pltpu.VMEM((1, D), f32),
            pltpu.VMEM((1, D), f32),
            pltpu.VMEM((ROWS * CACHE, HEAD_DIM), bf16),
            pltpu.VMEM((ROWS * CACHE, HEAD_DIM), bf16),
            pltpu.VMEM((ROWS, HEAD_DIM), f32),
            pltpu.VMEM((ROWS, HEAD_DIM), f32),
            pltpu.VMEM((ROWS, 1), jnp.int32),
            pltpu.VMEM((8, ROWS, K), bf16),
            pltpu.VMEM((8, 32, WC), bf16),
            pltpu.VMEM((8, 32, QC), bf16),
            pltpu.VMEM((4, 8, 32, WC), bf16),
            pltpu.VMEM((4, 8, 32, QC), bf16),
            pltpu.VMEM((8, ROWS, K), bf16),
            pltpu.VMEM((8, ROWS, WC), bf16),
            pltpu.VMEM((2, 4, ROWS, WC), bf16),
            pltpu.VMEM((ROWS, WC), f32),
            pltpu.VMEM((ROWS // BLOCK_ROWS, BLOCK_ROWS * GROUP, BLOCK_ROWS * CACHE), bf16),
            pltpu.VMEM((ROWS, QC), f32),
            pltpu.VMEM((8, ROWS, QC), bf16),
            pltpu.VMEM((2, 512, 512), bf16),
            pltpu.VMEM((2, 512, 512), bf16),
            pltpu.VMEM((2, 512, 512), f32),
            pltpu.VMEM((4, 1024, 128), bf16),
            pltpu.VMEM((4, 1024, 128), bf16),
            pltpu.VMEM((8, ROWS, 128), bf16),
            pltpu.VMEM((8, ROWS, 128), bf16),
            pltpu.VMEM((4, 2, 8, ROWS, 128), bf16),
            pltpu.VMEM((16, D), f32),
            pltpu.VMEM((ROWS, D), bf16),
            pltpu.VMEM((ROWS, D), bf16),
            pltpu.VMEM((ROWS, HEAD_DIM), bf16),
            pltpu.VMEM((ROWS, HEAD_DIM), bf16),
            dma((12,)),
            dma((4,)),
            dma((8,)),
            dma((8,)),
            dma((8, 4)),
            dma((8, 4)),
            dma((8,)),
            dma((8,)),
            dma((8, 4)),
            dma((8, 4)),
            dma((2, 4)),
            dma((2, 4)),
            dma((2, 4)),
            dma((2, 4)),
            dma((2, 4)),
            dma((2, 4)),
            dma((2, 4)),
            dma((2, 4)),
            dma((2,)),
            dma((2,)),
            dma((4,)),
            dma((4,)),
            dma((2, 4)),
            dma((2, 4)),
            dma((4,)),
            dma((4,)),
            dma((4,)),
            dma((4,)),
        ],
        compiler_params=pltpu.CompilerParams(collective_id=0, has_side_effects=True),
    )(
        hidden,
        q_weight,
        k_weight,
        v_weight,
        o_weight,
        input_gain.reshape(1, D),
        post_gain.reshape(1, D),
        kc,
        vc,
        cos,
        sin,
        lens,
    )
    return (
        new_hidden,
        normed,
        fresh.reshape(ROWS, 1, HEAD_DIM),
        values.reshape(ROWS, 1, HEAD_DIM),
    )


def solution(mesh):
    in_specs = (
        P("dp", None),
        P(("dp", "tensor"), None),
        P(("dp", "tensor"), None),
        P(("dp", "tensor"), None),
        P(("dp", "tensor"), None),
        P(),
        P(),
        P("dp", None, "tensor", None),
        P("dp", None, "tensor", None),
        P("dp"),
    )
    out_specs = (P("dp", None), P("dp", None), P("dp", "tensor", None), P("dp", "tensor", None))
    return jax.shard_map(shards, mesh=mesh, in_specs=in_specs, out_specs=out_specs, check_vma=False)
```

time: 505 us -> 155 us (0.31)
  waiting for transfers between devices: 404 us -> 0 us
  Pallas kernels: 0 us -> 145 us
  blocking collectives: 29.9 us -> 0 us
  matrix products: 23.5 us -> 0 us
  other arithmetic: 16.3 us -> 1.73 us
  starting transfers between devices: 14.1 us -> 0 us
  between operations: 13.9 us -> 0.66 us
  local copies, waits for them, and re-layouts: 1.81 us -> 7.18 us
    all_gather x2 -> x0, waiting for transfers between devices: 287 us -> none  [the longest x1 148 us: shards(): lax.all_gather(w_out, 'dp', axis=0, tiled=True)]
    pallas_call x0 -> x1, Pallas kernels: none -> 145 us  [shards(): pl.pallas_call(kernel, out_shape=(jax.ShapeDtypeStruct((ROWS, D), bf16),...]
    psum x1 -> x0, waiting for transfers between devices: 104 us -> none  [shards(): lax.psum(partial_value.astype(jnp.bfloat16), 'tensor').astype(jnp.float32)]
    all_to_all x2 -> x0, blocking collectives: 29.9 us -> none  [the longest x1 17.4 us: shards(): lax.all_to_all(o_weight.astype(jnp.bfloat16), 'tensor', split_axis=1, con...]
    dot_general x6 -> x0, matrix products: 23.5 us -> none  [the longest x3 12.3 us: shards(): jnp.dot(normal_in, portion, preferred_element_type=jnp.float32)]
    all_to_all x2 -> x0, starting transfers between devices: 14 us -> none  [the longest x1 9.95 us: shards(): lax.all_to_all(k_weight.astype(jnp.bfloat16), 'tensor', split_axis=1, con...]
    all_to_all x2 -> x0, waiting for transfers between devices: 12.5 us -> none  [the longest x1 6.48 us: shards(): lax.all_to_all(v_weight.astype(jnp.bfloat16), 'tensor', split_axis=1, con...]
    reduce_sum x3 -> x0, other arithmetic: 5.6 us -> none  [the longest x2 5.22 us: rms_gain(): mean_square = jnp.mean(values * values, axis=-1, keepdims=True)]
  transfers between devices with their start and end apart: 5 -> 0, of which waited for: 5 -> 0; matrix products, arithmetic and copies ran while one was open for 5% -> 0% of each run, Pallas kernels for 0% -> 0%
where the time goes in v1:
time: 155 us
  Pallas kernels  145 us (94%)
  local copies, waits for them, and re-layouts  7.18 us (5%)
  other arithmetic  1.73 us (1%)
    pallas_call x1, Pallas kernels, shards(): pl.pallas_call(kernel, out_shape=(jax.ShapeDtypeStruct((ROWS, D), bf16),...  145 us
    unnamed x10, local copies, waits for them, and re-layouts  5.8 us

profile of v1, /device:TPU:1, one launch (start us, length us, event | category | flops | bytes accessed | tf_op | source)
XLA Modules:
  0.0 154.9 jit_solution(1284954241561401303)
XLA Ops:
  0.6 0.7 convert_element_type.3
  1.3 1.4 copy.14.len_in
  2.7 0.3 fusion
  3.0 0.8 pad_maximum_fusion
  3.8 145.3 %shard_map.129 = (bf16[128,8192]{1,0:T(8,128)(2,1)}, bf16[128,8192]{1,0:T(8,128)(2,1)}, bf16[128,128]{1,0:T(8,128)(2,1)}, bf16[128,128]{1,0:T(8,128)(2,1)}) custom-call(bf16[128,8192]{1,0:T(8,128)(2,1)} %hidden_in.1, f32[32,4096]{1,0:T(8,128)} %qw_in.1, f32[32,1024]{1,0:T(8,128)} %kw_in.1, f32[32,1024]{1,0:T(8,128)} %vw_in.1, f32[32,4096]{1,0:T(8,128)} %ow_in.1, ...), custom_call_target="tpu_custom_call" | custom-call | tf_op jit(solution)/shard_map/pallas_call | solution.py:507
  149.0 0.0 copy-start
  149.0 3.2 %copy.19 = bf16[128,8192]{1,0:T(8,128)(2,1)} copy(bf16[128,8192]{1,0:T(8,128)(2,1)} %get-tuple-element.21) | data formatting | bytes 4194304
  152.3 0.0 copy-done
  152.3 0.0 copy-start.2
  152.3 0.0 copy-start.1
  152.3 1.3 copy.20
  153.6 0.0 copy-done.2
  153.6 0.6 copy.21
  154.2 0.0 copy-done.1
  154.2 0.6 copy.22
  (1 shorter events, 0.0 us)
Async XLA Ops:
  149.0 3.3 %copy-start = (bf16[128,8192]{1,0:T(8,128)(2,1)S(1)}, bf16[128,8192]{1,0:T(8,128)(2,1)}, u32[]{:S(2)}) copy-start(bf16[128,8192]{1,0:T(8,128)(2,1)} %get-tuple-element.22) | copy-start | bytes 6291460
  152.3 1.3 copy-start.2
  152.3 1.9 %copy-start.1 = (bf16[128,128]{1,0:T(8,128)(2,1)S(1)}, bf16[128,128]{1,0:T(8,128)(2,1)}, u32[]{:S(2)}) copy-start(bf16[128,128]{1,0:T(8,128)(2,1)} %get-tuple-element.11) | copy-start | bytes 98308

commit v2 on v0

v2 whole, which is shorter than its diff:
```python
import math

import jax
import jax.numpy as jnp
from jax import lax
from jax.experimental import pallas as pl
from jax.experimental.pallas import tpu as pltpu
from jax.sharding import PartitionSpec as P

HEAD_DIM = 128
GROUP = 4
ROWS = 128
D = 8192
CACHE = 64
QD = 4096
QC = GROUP * HEAD_DIM
WC = QC + 2 * HEAD_DIM
K = 1024
BLOCK_ROWS = 8
CHUNKS = 2
CR = ROWS // CHUNKS
CH = CR // 2
FEATURES = 256
FLIGHTS = 160

epsilon = 1e-05
rope_base = 500000.0

PEERS = [(1, 0), (1, 1), (1, 3), (1, 2), (0, 1), (0, 3), (0, 2)]


def kernel(
    hidden_in,
    qw_in,
    kw_in,
    vw_in,
    ow_in,
    gain_in,
    kc_in,
    vc_in,
    len_in,
    mixed_out,
    fresh_out,
    value_out,
    hidden,
    qw,
    kw,
    vw,
    ow,
    gain,
    kc,
    vc,
    len_row,
    lens,
    cos,
    sin,
    xn,
    wst,
    wg,
    og,
    a,
    pst,
    cx,
    cn,
    cf,
    zst,
    zrecv,
    own,
    probs,
    att32,
    attg,
    made,
    gall,
    fresh_v,
    value_v,
    in_sem,
    out_sem,
    send_sem,
    recv_sem,
):
    dp = lax.axis_index("dp")
    t = lax.axis_index("tensor")
    y = dp % 4
    x = (dp // 4) % 4
    zl = dp // 16
    k = dp // 4
    zh = t // 2
    c = t % 2
    mate = t + 1 - 2 * c

    def member(dz, i):
        return ((zl + dz) % 2) * 4 + (x + i) % 4

    def source(dz, i):
        return ((zl + dz) % 2) * 4 + (x - i + 4) % 4

    def shifted(dz):
        if dz == 0:
            return t
        return ((zh - c * (1 - 2 * zl) + 4) % 4) * 2 + c

    def along_x(i):
        return (zl * 4 + (x + i) % 4) * 4 + y

    def along_y(i):
        return k * 4 + (y + i) % 4

    def along_z(j):
        return ((zh + j) % 4) * 2 + c

    across = ((1 - zl) * 4 + x) * 4 + y

    sent = []

    def send(src, dst, to_dp, to_tensor):
        n = len(sent)
        copy = pltpu.make_async_remote_copy(
            src_ref=src,
            dst_ref=dst,
            send_sem=send_sem.at[n],
            recv_sem=recv_sem.at[n],
            device_id={"dp": to_dp, "tensor": to_tensor},
            device_id_type=pl.DeviceIdType.MESH,
        )
        copy.start()
        sent.append(copy)
        return copy

    loads = [
        pltpu.make_async_copy(src, dst, in_sem.at[n])
        for n, (src, dst) in enumerate(
            (
                (qw_in, qw),
                (kw_in, kw),
                (vw_in, vw),
                (hidden_in, hidden),
                (gain_in, gain),
                (len_in, len_row),
                (ow_in, ow),
                (kc_in, kc),
                (vc_in, vc),
            )
        )
    ]
    for copy in loads:
        copy.start()

    barrier = pltpu.get_barrier_semaphore()
    greeted = [(along_x(i), t) for i in range(1, 4)]
    greeted += [(across, t)]
    greeted += [(member(1, i) * 4 + y, shifted(1)) for i in range(4)]
    greeted += [(dp, (t + j) % 8) for j in range(1, 8)]
    greeted += [(along_y(i), t) for i in range(1, 4)]
    for peer in greeted:
        pl.semaphore_signal(
            barrier,
            inc=1,
            device_id={"dp": peer[0], "tensor": peer[1]},
            device_id_type=pl.DeviceIdType.MESH,
        )

    for n in (0, 1, 2):
        loads[n].wait()
    for j in range(8):
        wst[j, :, :QC] = qw[:, j * QC : (j + 1) * QC].astype(jnp.bfloat16)
        wst[j, :, QC : QC + HEAD_DIM] = kw[:, j * HEAD_DIM : (j + 1) * HEAD_DIM].astype(
            jnp.bfloat16
        )
        wst[j, :, QC + HEAD_DIM :] = vw[:, j * HEAD_DIM : (j + 1) * HEAD_DIM].astype(jnp.bfloat16)
    wg[y, t] = wst[t]
    pl.semaphore_wait(barrier, len(greeted))

    b1 = {}
    for j in (4, 2, 6, 3, 5, 1, 7):
        to = (t + j) % 8
        b1[j] = send(wst.at[to], wg.at[y, t], dp, to)

    loads[3].wait()
    loads[4].wait()

    def norm_rows(n, carry):
        rows = pl.ds(pl.multiple_of(n * 16, 16), 16)
        values = hidden[rows, :].astype(jnp.float32)
        mean_square = jnp.mean(values * values, axis=-1, keepdims=True)
        normal = (values * lax.rsqrt(mean_square + epsilon) * gain[...]).astype(jnp.bfloat16)
        for m in range(8):
            xn[m, rows, :] = normal[:, m * K : (m + 1) * K]
        return carry

    lax.fori_loop(0, ROWS // 16, norm_rows, 0)

    mine = pl.ds(pl.multiple_of(c * 64, 64), 64)
    ac = {}
    for dz, i in PEERS:
        to = member(dz, i)
        ac[dz, i] = send(xn.at[to, mine], a.at[k, mine], to * 4 + y, shifted(dz))
    a[k] = xn[k]

    b2 = {}
    arrival = [0, 1, 7, 2, 6, 3, 5, 4]
    for j in arrival:
        if j:
            b1[j].wait_recv()
        at = wg.at[y, (t - j + 8) % 8]
        b2[j, 1] = send(at, at, along_y(1), t)
        b2[j, 3] = send(at, at, along_y(3), t)
    b3 = []
    for j in arrival:
        i = 1 + 2 * (j % 2)
        b2[j, i].wait_recv()
        at = wg.at[(y + 4 - i) % 4, (t - j + 8) % 8]
        b3.append(send(at, at, along_y(i), t))

    loads[5].wait()
    diagonal = lax.broadcasted_iota(jnp.int32, (ROWS, ROWS), 0) == lax.broadcasted_iota(
        jnp.int32, (ROWS, ROWS), 1
    )
    lengths = jnp.sum(
        jnp.where(diagonal, len_row[...].astype(jnp.float32), 0.0), axis=-1, keepdims=True
    )
    lens[...] = lengths
    lane = lax.broadcasted_iota(jnp.int32, (1, HEAD_DIM), 1)
    index_row = (lane % 64).astype(jnp.float32)
    frequency = jnp.exp(-math.log(rope_base) * index_row / 64)
    angle = lengths * frequency
    cos[...] = jnp.cos(angle)
    sin[...] = jnp.where(lane < 64, -1.0, 1.0) * jnp.sin(angle)

    af = []
    for dz, i in [(1, 0), (0, 1), (0, 3), (1, 1), (1, 3), (0, 2), (1, 2)]:
        ac[dz, i].wait_recv()
        at = a.at[source(dz, i), mine]
        af.append(send(at, at, dp, mate))

    for j in arrival:
        b2[j, 3 - 2 * (j % 2)].wait_recv()
    for copy in b3:
        copy.wait_recv()
    for copy in af:
        copy.wait_recv()

    weights = wg[...].reshape(K, WC)
    first, second = slice(0, 64), slice(64, 128)
    near = {}
    far = {}
    for dz in (1, 0):
        part = (zl + dz) % 2
        rows = a[pl.ds(part * 4, 4)].reshape(4 * ROWS, K)
        out = jnp.dot(rows, weights, preferred_element_type=jnp.float32).reshape(4, ROWS, WC)
        pst[dz] = out.astype(jnp.bfloat16)
        far[dz, 0] = send(pst.at[dz, (x + 2) % 4, first], cx.at[dz, 0], along_x(1), t)
        far[dz, 1] = send(pst.at[dz, (x + 2) % 4, second], cx.at[dz, 1], along_x(3), t)
        near[dz, 0, 1] = send(pst.at[dz, (x + 1) % 4, second], cn.at[dz, 0, 1], along_x(1), t)
        near[dz, 1, 0] = send(pst.at[dz, (x + 3) % 4, first], cn.at[dz, 1, 0], along_x(3), t)

    loads[6].wait()
    og[zl, y] = ow[...].astype(jnp.bfloat16)
    at = og.at[zl, y]
    o1 = send(at, at, across, t)
    o2 = [send(at, at, along_y(i), t) for i in (2, 1, 3)]

    for dz in (1, 0):
        far[dz, 0].wait_recv()
        cf[dz, 0] = (
            cx[dz, 0].astype(jnp.float32) + pst[dz, (x + 1) % 4, first].astype(jnp.float32)
        ).astype(jnp.bfloat16)
        near[dz, 0, 0] = send(cf.at[dz, 0], cn.at[dz, 0, 0], along_x(1), t)
        far[dz, 1].wait_recv()
        cf[dz, 1] = (
            cx[dz, 1].astype(jnp.float32) + pst[dz, (x + 3) % 4, second].astype(jnp.float32)
        ).astype(jnp.bfloat16)
        near[dz, 1, 1] = send(cf.at[dz, 1], cn.at[dz, 1, 1], along_x(3), t)

    o1.wait_recv()
    at = og.at[1 - zl, y]
    o2 += [send(at, at, along_y(i), t) for i in (2, 1, 3)]

    zc = []
    for h, rows in enumerate((first, second)):
        near[1, 0, h].wait_recv()
        near[1, 1, h].wait_recv()
        zst[rows, :] = (
            pst[1, x, rows].astype(jnp.float32)
            + cn[1, 0, h].astype(jnp.float32)
            + cn[1, 1, h].astype(jnp.float32)
        ).astype(jnp.bfloat16)
        zc.append(send(zst.at[rows], zrecv.at[rows], across, t))

    loads[7].wait()
    loads[8].wait()
    scale = 1.0 / math.sqrt(HEAD_DIM)
    wide = BLOCK_ROWS * CACHE
    tall = BLOCK_ROWS * GROUP
    row_of = lax.broadcasted_iota(jnp.int32, (tall, wide), 0) % BLOCK_ROWS
    column = lax.broadcasted_iota(jnp.int32, (tall, wide), 1)
    same = row_of == column // CACHE
    position = (column % CACHE).astype(jnp.float32)

    def attend(h):
        chunk = slice(h * CR, (h + 1) * CR)
        cosine = cos[chunk, :]
        sine = sin[chunk, :]
        for m in range(GROUP + 1):
            columns = slice(m * HEAD_DIM, (m + 1) * HEAD_DIM)
            head = own[chunk, columns]
            head = head * cosine + pltpu.roll(head, 64, 1) * sine
            own[chunk, columns] = head.astype(jnp.bfloat16).astype(jnp.float32)
        fresh_v[chunk, :] = own[chunk, QC : QC + HEAD_DIM].astype(jnp.bfloat16)
        value_b = own[chunk, QC + HEAD_DIM :].astype(jnp.bfloat16)
        value_v[chunk, :] = value_b
        own[chunk, QC + HEAD_DIM :] = value_b.astype(jnp.float32)
        for n in range(h * CR // BLOCK_ROWS, (h + 1) * CR // BLOCK_ROWS):
            rows = slice(n * BLOCK_ROWS, (n + 1) * BLOCK_ROWS)
            query = jnp.concatenate(
                [own[rows, m * HEAD_DIM : (m + 1) * HEAD_DIM] for m in range(GROUP)], axis=0
            )
            fresh = jnp.concatenate([own[rows, QC : QC + HEAD_DIM]] * GROUP, axis=0)
            length = jnp.concatenate([lens[rows, :]] * GROUP, axis=0)
            scores = (
                lax.dot_general(
                    query.astype(jnp.bfloat16),
                    kc[n * wide : (n + 1) * wide, :],
                    (((1,), (1,)), ((), ())),
                    preferred_element_type=jnp.float32,
                )
                * scale
            )
            self_score = jnp.sum(query * fresh, axis=-1, keepdims=True) * scale
            kept = same & (position < length)
            scores = jnp.where(kept, scores, -jnp.inf)
            largest = jnp.maximum(jnp.max(scores, axis=-1, keepdims=True), self_score)
            kept_exp = jnp.exp(scores - largest)
            own_exp = jnp.exp(self_score - largest)
            divisor = jnp.sum(kept_exp, axis=-1, keepdims=True) + own_exp
            probs[n] = (kept_exp / divisor).astype(jnp.bfloat16)
            own_prob = (own_exp / divisor).astype(jnp.bfloat16).astype(jnp.float32)
            value = jnp.concatenate([own[rows, QC + HEAD_DIM :]] * GROUP, axis=0)
            attended = (
                jnp.dot(
                    probs[n],
                    vc[n * wide : (n + 1) * wide, :],
                    preferred_element_type=jnp.float32,
                )
                + own_prob * value
            )
            for m in range(GROUP):
                att32[rows, m * HEAD_DIM : (m + 1) * HEAD_DIM] = attended[
                    m * BLOCK_ROWS : (m + 1) * BLOCK_ROWS
                ]

    def tq(d):
        return ((zh + d) % 4) * 2 + c

    def xq(i):
        return (x + i) % 4

    lower, upper = slice(0, CH), slice(CH, CR)
    z1, z2, x1, x2 = {}, {}, {}, {}
    to_mate = {n: [] for n in range(CHUNKS)}

    def hand(n, at):
        to_mate[n].append(send(at, at, dp, mate))

    def spread_x(n, d):
        at = attg.at[n, tq(d), x]
        x1[n, d, 1] = send(at, at, along_x(1), t)
        x1[n, d, 3] = send(at, at, along_x(3), t)
        hand(n, at)

    def z_first(n):
        z1[n, 1].wait_recv()
        at = attg.at[n, tq(3), x, lower]
        z2[n, 1] = send(at, at, dp, along_z(1))
        z1[n, 3].wait_recv()
        at = attg.at[n, tq(1), x, upper]
        z2[n, 3] = send(at, at, dp, along_z(3))
        spread_x(n, 3)
        spread_x(n, 1)

    def z_second(n):
        z2[n, 1].wait_recv()
        z2[n, 3].wait_recv()
        spread_x(n, 2)

    def x_first(n):
        for d in (0, 3, 1, 2):
            x1[n, d, 1].wait_recv()
            at = attg.at[n, tq(d), xq(3)]
            x2[n, d, 1] = send(at.at[lower], at.at[lower], along_x(1), t)
            hand(n, at)
            x1[n, d, 3].wait_recv()
            at = attg.at[n, tq(d), xq(1)]
            x2[n, d, 3] = send(at.at[upper], at.at[upper], along_x(3), t)
            hand(n, at)

    def x_second(n):
        for d in (0, 3, 1, 2):
            x2[n, d, 1].wait_recv()
            x2[n, d, 3].wait_recv()
            hand(n, attg.at[n, tq(d), xq(2)])

    for h, rows in enumerate((first, second)):
        near[0, 0, h].wait_recv()
        near[0, 1, h].wait_recv()
        own[rows, :] = (
            pst[0, x, rows].astype(jnp.float32)
            + cn[0, 0, h].astype(jnp.float32)
            + cn[0, 1, h].astype(jnp.float32)
        )
        zc[h].wait_recv()
        own[rows, :] += zrecv[rows, :].astype(jnp.float32)
        attend(h)
        attg[h, t, x] = att32[rows, :].astype(jnp.bfloat16)
        at = attg.at[h, t, x]
        z1[h, 1] = send(at, at, dp, along_z(1))
        z1[h, 3] = send(at, at, dp, along_z(3))
        spread_x(h, 0)

    z_first(0)
    z_first(1)
    z_second(0)
    z_second(1)

    tc, u1, u2 = {}, {}, {}
    final = {n: [] for n in range(CHUNKS)}

    def project(n):
        for copy in to_mate[n]:
            copy.wait_recv()
        out = jnp.zeros((4 * CR, FEATURES), jnp.float32)
        for j in range(8):
            out += lax.dot_general(
                attg[n, j].reshape(4 * CR, QC),
                og[:, :, :, j * QC : (j + 1) * QC].reshape(FEATURES, QC),
                (((1,), (1,)), ((), ())),
                preferred_element_type=jnp.float32,
            )
        made[n] = out.astype(jnp.bfloat16).reshape(4, CR, FEATURES)
        for i in (2, 1, 3):
            tc[n, i] = send(made.at[n, xq(i)], gall.at[n, t, x], along_x(i), t)
        gall[n, t, x] = made[n, x]

    def gather_first(n):
        for i in (1, 3, 2):
            tc[n, i].wait_recv()
        at = gall.at[n, t]
        u1[n, 1] = send(at, at, dp, along_z(1))
        u1[n, 3] = send(at, at, dp, along_z(3))
        final[n].append(send(at, at, dp, mate))

    def gather_second(n):
        u1[n, 1].wait_recv()
        at = gall.at[n, tq(3)]
        part = at.at[pl.ds(0, 2)]
        u2[n, 1] = send(part, part, dp, along_z(1))
        final[n].append(send(at, at, dp, mate))
        u1[n, 3].wait_recv()
        at = gall.at[n, tq(1)]
        part = at.at[pl.ds(2, 2)]
        u2[n, 3] = send(part, part, dp, along_z(3))
        final[n].append(send(at, at, dp, mate))

    def gather_third(n):
        u2[n, 1].wait_recv()
        u2[n, 3].wait_recv()
        at = gall.at[n, tq(2)]
        final[n].append(send(at, at, dp, mate))

    x_first(0)
    x_second(0)
    for copy in o2:
        copy.wait_recv()
    project(0)
    x_first(1)
    gather_first(0)
    x_second(1)
    project(1)
    gather_second(0)
    gather_first(1)
    gather_third(0)
    gather_second(1)
    stores = [
        pltpu.make_async_copy(src, dst, out_sem.at[n])
        for n, (src, dst) in enumerate(
            (
                (gall.at[0], mixed_out.at[0]),
                (gall.at[1], mixed_out.at[1]),
                (fresh_v, fresh_out),
                (value_v, value_out),
            )
        )
    ]
    stores[2].start()
    stores[3].start()
    for copy in final[0]:
        copy.wait_recv()
    stores[0].start()
    gather_third(1)
    for copy in final[1]:
        copy.wait_recv()
    stores[1].start()
    for copy in stores:
        copy.wait()
    for copy in sent:
        copy.wait_send()


def finish(hidden, mixed, fresh, value, post, new_hidden, normed, fresh_out, value_out, residual):
    lane = lax.broadcasted_iota(jnp.int32, (1, 128), 1)
    squares = jnp.zeros((16, 128), jnp.float32)
    for x in range(4):
        for q in range(2):
            for zl in range(2):
                pieces = [
                    mixed[0, 4 * q + s, x, :, zl * 128 : (zl + 1) * 128].astype(jnp.float32)
                    for s in range(4)
                ]
                turned = [pieces[0]] + [pltpu.roll(pieces[s], 32 * s, 1) for s in range(1, 4)]
                for y in range(4):
                    block = turned[(0 - y) % 4]
                    for p in range(1, 4):
                        block = jnp.where(lane // 32 == p, turned[(p - y) % 4], block)
                    if y:
                        block = pltpu.roll(block, 128 - 32 * y, 1)
                    at = (zl * 16 + x * 4 + y) * 256 + q * 128
                    columns = slice(at, at + 128)
                    total = hidden[:, columns].astype(jnp.float32) + block
                    new_hidden[:, columns] = total.astype(jnp.bfloat16)
                    residual[:, columns] = total
                    squares += total * total
    mean_square = jnp.sum(squares, axis=-1, keepdims=True) * (1.0 / D)
    normed[...] = (residual[...] * lax.rsqrt(mean_square + epsilon) * post[...]).astype(
        jnp.bfloat16
    )
    fresh_out[...] = fresh[...]
    value_out[...] = value[...]


def shards(
    hidden,
    q_weight,
    k_weight,
    v_weight,
    o_weight,
    input_gain,
    post_gain,
    key_cache,
    value_cache,
    lengths,
):
    kc = jnp.transpose(key_cache, (0, 2, 1, 3)).reshape(ROWS * CACHE, HEAD_DIM)
    vc = jnp.transpose(value_cache, (0, 2, 1, 3)).reshape(ROWS * CACHE, HEAD_DIM)
    bf16, f32 = jnp.bfloat16, jnp.float32
    dma = pltpu.SemaphoreType.DMA
    mixed, fresh, values = pl.pallas_call(
        kernel,
        out_shape=(
            jax.ShapeDtypeStruct((CHUNKS, 8, 4, CR, FEATURES), bf16),
            jax.ShapeDtypeStruct((ROWS, HEAD_DIM), bf16),
            jax.ShapeDtypeStruct((ROWS, HEAD_DIM), bf16),
        ),
        in_specs=[pl.BlockSpec(memory_space=pl.ANY)] * 9,
        out_specs=[pl.BlockSpec(memory_space=pl.ANY)] * 3,
        scratch_shapes=[
            pltpu.VMEM((ROWS, D), bf16),
            pltpu.VMEM((32, QD), f32),
            pltpu.VMEM((32, 1024), f32),
            pltpu.VMEM((32, 1024), f32),
            pltpu.VMEM((32, QD), f32),
            pltpu.VMEM((1, D), f32),
            pltpu.VMEM((ROWS * CACHE, HEAD_DIM), bf16),
            pltpu.VMEM((ROWS * CACHE, HEAD_DIM), bf16),
            pltpu.VMEM((1, ROWS), jnp.int32),
            pltpu.VMEM((ROWS, 1), f32),
            pltpu.VMEM((ROWS, HEAD_DIM), f32),
            pltpu.VMEM((ROWS, HEAD_DIM), f32),
            pltpu.VMEM((8, ROWS, K), bf16),
            pltpu.VMEM((8, 32, WC), bf16),
            pltpu.VMEM((4, 8, 32, WC), bf16),
            pltpu.VMEM((2, 4, 32, QD), bf16),
            pltpu.VMEM((8, ROWS, K), bf16),
            pltpu.VMEM((2, 4, ROWS, WC), bf16),
            pltpu.VMEM((2, 2, 64, WC), bf16),
            pltpu.VMEM((2, 2, 2, 64, WC), bf16),
            pltpu.VMEM((2, 2, 64, WC), bf16),
            pltpu.VMEM((ROWS, WC), bf16),
            pltpu.VMEM((ROWS, WC), bf16),
            pltpu.VMEM((ROWS, WC), f32),
            pltpu.VMEM((ROWS // BLOCK_ROWS, BLOCK_ROWS * GROUP, BLOCK_ROWS * CACHE), bf16),
            pltpu.VMEM((ROWS, QC), f32),
            pltpu.VMEM((CHUNKS, 8, 4, CR, QC), bf16),
            pltpu.VMEM((CHUNKS, 4, CR, FEATURES), bf16),
            pltpu.VMEM((CHUNKS, 8, 4, CR, FEATURES), bf16),
            pltpu.VMEM((ROWS, HEAD_DIM), bf16),
            pltpu.VMEM((ROWS, HEAD_DIM), bf16),
            dma((9,)),
            dma((4,)),
            dma((FLIGHTS,)),
            dma((FLIGHTS,)),
        ],
        compiler_params=pltpu.CompilerParams(collective_id=0, has_side_effects=True),
    )(
        hidden,
        q_weight,
        k_weight,
        v_weight,
        o_weight,
        input_gain.reshape(1, D),
        kc,
        vc,
        lengths.reshape(1, ROWS),
    )
    blocks = CR // 16
    wide = pl.BlockSpec((16, D), lambda n: (n, 0))
    narrow = pl.BlockSpec((16, HEAD_DIM), lambda n: (n, 0))
    new_hidden, normed, fresh, values = pl.pallas_call(
        finish,
        grid=(ROWS // 16,),
        out_shape=(
            jax.ShapeDtypeStruct((ROWS, D), bf16),
            jax.ShapeDtypeStruct((ROWS, D), bf16),
            jax.ShapeDtypeStruct((ROWS, HEAD_DIM), bf16),
            jax.ShapeDtypeStruct((ROWS, HEAD_DIM), bf16),
        ),
        in_specs=[
            wide,
            pl.BlockSpec((1, 8, 4, 16, FEATURES), lambda n: (n // blocks, 0, 0, n % blocks, 0)),
            narrow,
            narrow,
            pl.BlockSpec((1, D), lambda n: (0, 0)),
        ],
        out_specs=[wide, wide, narrow, narrow],
        scratch_shapes=[pltpu.VMEM((16, D), f32)],
    )(hidden, mixed, fresh, values, post_gain.reshape(1, D))
    return (
        new_hidden,
        normed,
        fresh.reshape(ROWS, 1, HEAD_DIM),
        values.reshape(ROWS, 1, HEAD_DIM),
    )


def solution(mesh):
    in_specs = (
        P("dp", None),
        P(("dp", "tensor"), None),
        P(("dp", "tensor"), None),
        P(("dp", "tensor"), None),
        P(("dp", "tensor"), None),
        P(),
        P(),
        P("dp", None, "tensor", None),
        P("dp", None, "tensor", None),
        P("dp"),
    )
    out_specs = (P("dp", None), P("dp", None), P("dp", "tensor", None), P("dp", "tensor", None))
    return jax.shard_map(shards, mesh=mesh, in_specs=in_specs, out_specs=out_specs, check_vma=False)
```

time: 505 us -> 115 us (0.23)
  waiting for transfers between devices: 404 us -> 0 us
  Pallas kernels: 0 us -> 114 us
  blocking collectives: 29.9 us -> 0 us
  matrix products: 23.5 us -> 0 us
  other arithmetic: 16.3 us -> 0 us
  starting transfers between devices: 14.1 us -> 0 us
  between operations: 13.9 us -> 0.64 us
    all_gather x2 -> x0, waiting for transfers between devices: 287 us -> none  [the longest x1 148 us: shards(): lax.all_gather(w_out, 'dp', axis=0, tiled=True)]
    pallas_call x0 -> x2, Pallas kernels: none -> 114 us  [the longest x1 106 us: shards(): pl.pallas_call(kernel, out_shape=(jax.ShapeDtypeStruct((CHUNKS, 8, 4, CR,...]
    psum x1 -> x0, waiting for transfers between devices: 104 us -> none  [shards(): lax.psum(partial_value.astype(jnp.bfloat16), 'tensor').astype(jnp.float32)]
    all_to_all x2 -> x0, blocking collectives: 29.9 us -> none  [the longest x1 17.4 us: shards(): lax.all_to_all(o_weight.astype(jnp.bfloat16), 'tensor', split_axis=1, con...]
    dot_general x6 -> x0, matrix products: 23.5 us -> none  [the longest x3 12.3 us: shards(): jnp.dot(normal_in, portion, preferred_element_type=jnp.float32)]
    all_to_all x2 -> x0, starting transfers between devices: 14 us -> none  [the longest x1 9.95 us: shards(): lax.all_to_all(k_weight.astype(jnp.bfloat16), 'tensor', split_axis=1, con...]
    all_to_all x2 -> x0, waiting for transfers between devices: 12.5 us -> none  [the longest x1 6.48 us: shards(): lax.all_to_all(v_weight.astype(jnp.bfloat16), 'tensor', split_axis=1, con...]
    reduce_sum x3 -> x0, other arithmetic: 5.6 us -> none  [the longest x2 5.22 us: rms_gain(): mean_square = jnp.mean(values * values, axis=-1, keepdims=True)]
  transfers between devices with their start and end apart: 5 -> 0, of which waited for: 5 -> 0; matrix products, arithmetic and copies ran while one was open for 5% -> 0% of each run, Pallas kernels for 0% -> 0%
where the time goes in v2:
time: 115 us
  Pallas kernels  114 us (99%)
    pallas_call x1, Pallas kernels, shards(): pl.pallas_call(kernel, out_shape=(jax.ShapeDtypeStruct((CHUNKS, 8, 4, CR,...  106 us
    pallas_call x1, Pallas kernels, shards(): pl.pallas_call(finish, grid=(ROWS // 16,), out_shape=(jax.ShapeDtypeStruc...  7.67 us

profile of v2, /device:TPU:1, one launch (start us, length us, event | category | flops | bytes accessed | tf_op | source)
XLA Modules:
  0.0 114.5 jit_solution(13395824178344900907)
XLA Ops:
  0.6 106.2 %shard_map.129 = (bf16[2,8,4,64,256]{4,3,2,1,0:T(8,128)(2,1)}, bf16[128,128]{1,0:T(8,128)(2,1)}, bf16[128,128]{1,0:T(8,128)(2,1)}) custom-call(bf16[128,8192]{1,0:T(8,128)(2,1)} %hidden.1, f32[32,4096]{1,0:T(8,128)} %qw_in.1, f32[32,1024]{1,0:T(8,128)} %kw_in.1, f32[32,1024]{1,0:T(8,128)} %vw_in.1, f32[32,4096]{1,0:T(8,128)} %ow_in.1, f32[1,8192]{1,0:T(1,128)} %bitcast.9, ...), custom_call_target="tpu_custom_call" | custom-call | tf_op jit(solution)/shard_map/pallas_call | solution.py:555
  106.8 7.7 %shard_map.130 = (bf16[128,8192]{1,0:T(8,128)(2,1)}, bf16[128,8192]{1,0:T(8,128)(2,1)}, bf16[128,128]{1,0:T(8,128)(2,1)}, bf16[128,128]{1,0:T(8,128)(2,1)}) custom-call(bf16[128,8192]{1,0:T(8,128)(2,1)} %hidden.1, bf16[2,8,4,64,256]{4,3,2,1,0:T(8,128)(2,1)} %get-tuple-element.11.mixed, bf16[128,128]{1,0:T(8,128)(2,1)} %get-tuple-element.12.fresh, ...), custom_call_target="tpu_custom_call" | custom-call | tf_op jit(solution)/shard_map/pallas_call | solution.py:616

commit v3 on v2

v3 whole, which is shorter than its diff:
```python
import math

import jax
import jax.numpy as jnp
from jax import lax
from jax.experimental import pallas as pl
from jax.experimental.pallas import tpu as pltpu
from jax.sharding import PartitionSpec as P

HEAD_DIM = 128
GROUP = 4
ROWS = 128
D = 8192
CACHE = 64
QD = 4096
QC = GROUP * HEAD_DIM
WC = QC + 2 * HEAD_DIM
K = 1024
BLOCK_ROWS = 8
CHUNKS = 4
CR = ROWS // CHUNKS
CH = CR // 2
HALF = ROWS // 2
QUARTER = ROWS // 4
FEATURES = 256
SENDS = 32
RECEIVES = 128

epsilon = 1e-05
rope_base = 500000.0

PEERS = [(1, 0), (1, 1), (1, 3), (1, 2), (0, 1), (0, 3), (0, 2)]


def kernel(
    hidden_in,
    qw_in,
    kw_in,
    vw_in,
    ow_in,
    gain_in,
    post_in,
    kc_in,
    vc_in,
    len_in,
    new_out,
    normed_out,
    fresh_out,
    value_out,
    hidden,
    qw,
    kw,
    vw,
    ow,
    gain,
    post,
    kc,
    vc,
    len_row,
    lens,
    cos,
    sin,
    xn,
    wst,
    wg,
    og,
    a,
    acc,
    pst,
    cx,
    cn,
    cf,
    zst,
    zrecv,
    own,
    probs,
    att32,
    attg,
    made,
    gall,
    turn,
    runs,
    ordered,
    residual,
    new_v,
    normed_v,
    fresh_v,
    value_v,
    in_sem,
    out_sem,
    send_sem,
    recv_sem,
):
    dp = lax.axis_index("dp")
    t = lax.axis_index("tensor")
    y = dp % 4
    x = (dp // 4) % 4
    zl = dp // 16
    k = dp // 4
    zh = t // 2
    c = t % 2
    mate = t + 1 - 2 * c

    def member(dz, i):
        return ((zl + dz) % 2) * 4 + (x + i) % 4

    def source(dz, i):
        return ((zl + dz) % 2) * 4 + (x - i + 4) % 4

    def shifted(dz):
        if dz == 0:
            return t
        return ((zh - c * (1 - 2 * zl) + 4) % 4) * 2 + c

    def along_x(i):
        return (zl * 4 + (x + i) % 4) * 4 + y

    def along_y(i):
        return k * 4 + (y + i) % 4

    def along_z(j):
        return ((zh + j) % 4) * 2 + c

    across = ((1 - zl) * 4 + x) * 4 + y

    out_groups, in_groups, out_size, in_size = {}, {}, {}, {}

    def describe(src, dst, out_key, in_key, to_dp, to_tensor):
        n = out_groups.setdefault(out_key, len(out_groups))
        m = in_groups.setdefault(in_key, len(in_groups))
        assert n < SENDS and m < RECEIVES
        return pltpu.make_async_remote_copy(
            src_ref=src,
            dst_ref=dst,
            send_sem=send_sem.at[n],
            recv_sem=recv_sem.at[m],
            device_id={"dp": to_dp, "tensor": to_tensor},
            device_id_type=pl.DeviceIdType.MESH,
        )

    def send(src, dst, out_key, in_key, to_dp, to_tensor):
        size = math.prod(src.shape)
        assert size == math.prod(dst.shape)
        out_size[out_key] = out_size.get(out_key, 0) + size
        in_size[in_key] = in_size.get(in_key, 0) + size
        describe(src, dst, out_key, in_key, to_dp, to_tensor).start()

    def received(in_key, ref):
        assert in_size.pop(in_key) == math.prod(ref.shape)
        describe(ref, ref, next(iter(out_groups)), in_key, dp, mate).wait_recv()

    def departed(out_key, ref):
        assert out_size.pop(out_key) == math.prod(ref.shape)
        describe(ref, ref, out_key, next(iter(in_groups)), dp, mate).wait_send()

    loads = [
        pltpu.make_async_copy(src, dst, in_sem.at[n])
        for n, (src, dst) in enumerate(
            (
                (qw_in, qw),
                (kw_in, kw),
                (vw_in, vw),
                (hidden_in, hidden),
                (gain_in, gain),
                (len_in, len_row),
                (ow_in, ow),
                (kc_in, kc),
                (vc_in, vc),
                (post_in, post),
            )
        )
    ]
    for copy in loads:
        copy.start()

    barrier = pltpu.get_barrier_semaphore()
    greeted = [(along_x(i), t) for i in range(1, 4)]
    greeted += [(across, t)]
    greeted += [(member(1, i) * 4 + y, shifted(1)) for i in range(4)]
    greeted += [(dp, (t + j) % 8) for j in range(1, 8)]
    greeted += [(along_y(i), t) for i in range(1, 4)]
    for peer in greeted:
        pl.semaphore_signal(
            barrier,
            inc=1,
            device_id={"dp": peer[0], "tensor": peer[1]},
            device_id_type=pl.DeviceIdType.MESH,
        )

    for n in (0, 1, 2):
        loads[n].wait()
    for j in range(8):
        wst[j, :, :QC] = qw[:, j * QC : (j + 1) * QC].astype(jnp.bfloat16)
        wst[j, :, QC : QC + HEAD_DIM] = kw[:, j * HEAD_DIM : (j + 1) * HEAD_DIM].astype(
            jnp.bfloat16
        )
        wst[j, :, QC + HEAD_DIM :] = vw[:, j * HEAD_DIM : (j + 1) * HEAD_DIM].astype(jnp.bfloat16)
    wg[y, t] = wst[t]
    pl.semaphore_wait(barrier, len(greeted))

    pieces = [(0, 1), (1, 0), (3, 0), (1, 1), (3, 1), (2, 0), (2, 1)]
    for j, i in pieces:
        to = ((zh + j) % 4) * 2 + (c + i) % 2
        send(wst.at[to], wg.at[y, t], "b1", ("b1", j, i), dp, to)

    loads[3].wait()
    loads[4].wait()

    def norm_rows(n, carry):
        rows = pl.ds(pl.multiple_of(n * 16, 16), 16)
        values = hidden[rows, :].astype(jnp.float32)
        mean_square = jnp.mean(values * values, axis=-1, keepdims=True)
        normal = (values * lax.rsqrt(mean_square + epsilon) * gain[...]).astype(jnp.bfloat16)
        for m in range(8):
            xn[m, rows, :] = normal[:, m * K : (m + 1) * K]
        return carry

    lax.fori_loop(0, ROWS // 16, norm_rows, 0)

    mine = pl.ds(pl.multiple_of(c * HALF, HALF), HALF)
    for dz, i in PEERS:
        to = member(dz, i)
        send(xn.at[to, mine], a.at[k, mine], "a", ("a", dz, i), to * 4 + y, shifted(dz))
    a[k] = xn[k]

    arrival = [(0, 0)] + pieces
    for n, (j, i) in enumerate(arrival):
        at = wg.at[y, ((zh - j + 4) % 4) * 2 + (c + i) % 2]
        if n:
            received(("b1", j, i), at)
        if n % 2:
            send(at, at, "b", "b2", along_y(1), t)
            send(at, at, "b", ("b2", n), along_y(3), t)
        else:
            send(at, at, "b", ("b2", n), along_y(1), t)
            send(at, at, "b", "b2", along_y(3), t)

    loads[6].wait()
    og[zl, y] = ow[...].astype(jnp.bfloat16)
    at = og.at[zl, y]
    send(at, at, "o1", "o1", across, t)

    for n, (j, i) in enumerate(arrival):
        way = 1 + 2 * (n % 2)
        at = wg.at[(y + 4 - way) % 4, ((zh - j + 4) % 4) * 2 + (c + i) % 2]
        received(("b2", n), at)
        send(at, at, "b", "b3", along_y(way), t)

    loads[5].wait()
    diagonal = lax.broadcasted_iota(jnp.int32, (ROWS, ROWS), 0) == lax.broadcasted_iota(
        jnp.int32, (ROWS, ROWS), 1
    )
    lengths = jnp.sum(
        jnp.where(diagonal, len_row[...].astype(jnp.float32), 0.0), axis=-1, keepdims=True
    )
    lens[...] = lengths
    lane = lax.broadcasted_iota(jnp.int32, (1, HEAD_DIM), 1)
    index_row = (lane % 64).astype(jnp.float32)
    frequency = jnp.exp(-math.log(rope_base) * index_row / 64)
    angle = lengths * frequency
    cos[...] = jnp.cos(angle)
    sin[...] = jnp.where(lane < 64, -1.0, 1.0) * jnp.sin(angle)

    down = lax.broadcasted_iota(jnp.int32, (512, 512), 0)
    over = lax.broadcasted_iota(jnp.int32, (512, 512), 1)
    turn[...] = jnp.where(
        (down // 128 == (over // 32) % 4)
        & ((down // 32) % 4 == over // 128)
        & (down % 32 == over % 32),
        1.0,
        0.0,
    ).astype(jnp.bfloat16)

    for dz, i in [(1, 0), (0, 1), (0, 3), (1, 1), (1, 3), (0, 2), (1, 2)]:
        at = a.at[source(dz, i), mine]
        received(("a", dz, i), at)
        send(at, at, "a", "af", dp, mate)
    received("af", a.at[0:7, 0:HALF])
    received("b2", wg.at[0])

    units = [(0, 1), (0, 0), (1, 1), (1, 0)]

    def product(h, dz, i):
        part = (zl + dz) % 2
        at = (y + i) % 4
        rows = a[
            pl.ds(part * 4, 4),
            h * HALF : (h + 1) * HALF,
            pl.ds(pl.multiple_of(at * 256, 256), 256),
        ]
        return jnp.dot(
            rows.reshape(4 * HALF, 256),
            wg[at].reshape(256, WC),
            preferred_element_type=jnp.float32,
        )

    for h, dz in units:
        acc[h, dz] = product(h, dz, 0) + product(h, dz, 1) + product(h, dz, 3)
    received("b3", wg.at[0])

    upper_rows, lower_rows = slice(0, QUARTER), slice(QUARTER, HALF)

    def multiply(h, dz):
        pst[h, dz] = (
            (acc[h, dz] + product(h, dz, 2)).astype(jnp.bfloat16).reshape(4, HALF, WC)
        )

    def depart(h, dz):
        far = (x + 2) % 4
        send(pst.at[h, dz, far, upper_rows], cx.at[h, dz, 0], "c", ("far", h, dz, 0), along_x(1), t)
        send(pst.at[h, dz, far, lower_rows], cx.at[h, dz, 1], "c", ("far", h, dz, 1), along_x(3), t)
        send(
            pst.at[h, dz, (x + 1) % 4, lower_rows],
            cn.at[h, dz, 0, 1],
            "c",
            ("near", h, dz),
            along_x(1),
            t,
        )
        send(
            pst.at[h, dz, (x + 3) % 4, upper_rows],
            cn.at[h, dz, 1, 0],
            "c",
            ("near", h, dz),
            along_x(3),
            t,
        )

    def forward(h, dz):
        for side, rows in enumerate((upper_rows, lower_rows)):
            way = 1 + 2 * side
            received(("far", h, dz, side), cx.at[h, dz, side])
            cf[h, dz, side] = (
                cx[h, dz, side].astype(jnp.float32)
                + pst[h, dz, (x + way) % 4, rows].astype(jnp.float32)
            ).astype(jnp.bfloat16)
            send(
                cf.at[h, dz, side],
                cn.at[h, dz, side, side],
                "c",
                ("near", h, dz),
                along_x(way),
                t,
            )

    def summed(h, dz):
        received(("near", h, dz), cn.at[h, dz])
        return (
            pst[h, dz, x].astype(jnp.float32)
            + cn[h, dz, 0].reshape(HALF, WC).astype(jnp.float32)
            + cn[h, dz, 1].reshape(HALF, WC).astype(jnp.float32)
        )

    def cross(h):
        zst[h] = summed(h, 1).astype(jnp.bfloat16)
        send(zst.at[h], zrecv.at[h], "z", ("z", h), across, t)

    def collect(h):
        total = summed(h, 0)
        received(("z", h), zrecv.at[h])
        own[h * HALF : (h + 1) * HALF, :] = total + zrecv[h].astype(jnp.float32)

    multiply(0, 1)
    depart(0, 1)
    multiply(0, 0)
    depart(0, 0)
    multiply(1, 1)
    forward(0, 1)
    depart(1, 1)
    multiply(1, 0)
    forward(0, 0)
    depart(1, 0)
    at = og.at[zl, y]
    for i in (2, 1, 3):
        send(at, at, "o2", "o2", along_y(i), t)
    at = og.at[1 - zl, y]
    received("o1", at)
    for i in (2, 1, 3):
        send(at, at, "o2", "o2", along_y(i), t)
    for n in (7, 8, 9):
        loads[n].wait()

    scale = 1.0 / math.sqrt(HEAD_DIM)
    wide = BLOCK_ROWS * CACHE
    tall = BLOCK_ROWS * GROUP
    row_of = lax.broadcasted_iota(jnp.int32, (tall, wide), 0) % BLOCK_ROWS
    column = lax.broadcasted_iota(jnp.int32, (tall, wide), 1)
    same = row_of == column // CACHE
    position = (column % CACHE).astype(jnp.float32)

    def attend(h):
        chunk = slice(h * CR, (h + 1) * CR)
        cosine = cos[chunk, :]
        sine = sin[chunk, :]
        for m in range(GROUP + 1):
            columns = slice(m * HEAD_DIM, (m + 1) * HEAD_DIM)
            head = own[chunk, columns]
            head = head * cosine + pltpu.roll(head, 64, 1) * sine
            own[chunk, columns] = head.astype(jnp.bfloat16).astype(jnp.float32)
        fresh_v[chunk, :] = own[chunk, QC : QC + HEAD_DIM].astype(jnp.bfloat16)
        value_b = own[chunk, QC + HEAD_DIM :].astype(jnp.bfloat16)
        value_v[chunk, :] = value_b
        own[chunk, QC + HEAD_DIM :] = value_b.astype(jnp.float32)
        for n in range(h * CR // BLOCK_ROWS, (h + 1) * CR // BLOCK_ROWS):
            rows = slice(n * BLOCK_ROWS, (n + 1) * BLOCK_ROWS)
            query = jnp.concatenate(
                [own[rows, m * HEAD_DIM : (m + 1) * HEAD_DIM] for m in range(GROUP)], axis=0
            )
            fresh = jnp.concatenate([own[rows, QC : QC + HEAD_DIM]] * GROUP, axis=0)
            length = jnp.concatenate([lens[rows, :]] * GROUP, axis=0)
            scores = (
                lax.dot_general(
                    query.astype(jnp.bfloat16),
                    kc[n * wide : (n + 1) * wide, :],
                    (((1,), (1,)), ((), ())),
                    preferred_element_type=jnp.float32,
                )
                * scale
            )
            self_score = jnp.sum(query * fresh, axis=-1, keepdims=True) * scale
            kept = same & (position < length)
            scores = jnp.where(kept, scores, -jnp.inf)
            largest = jnp.maximum(jnp.max(scores, axis=-1, keepdims=True), self_score)
            kept_exp = jnp.exp(scores - largest)
            own_exp = jnp.exp(self_score - largest)
            divisor = jnp.sum(kept_exp, axis=-1, keepdims=True) + own_exp
            probs[n] = (kept_exp / divisor).astype(jnp.bfloat16)
            own_prob = (own_exp / divisor).astype(jnp.bfloat16).astype(jnp.float32)
            value = jnp.concatenate([own[rows, QC + HEAD_DIM :]] * GROUP, axis=0)
            attended = (
                jnp.dot(
                    probs[n],
                    vc[n * wide : (n + 1) * wide, :],
                    preferred_element_type=jnp.float32,
                )
                + own_prob * value
            )
            for m in range(GROUP):
                att32[rows, m * HEAD_DIM : (m + 1) * HEAD_DIM] = attended[
                    m * BLOCK_ROWS : (m + 1) * BLOCK_ROWS
                ]
        attg[h, t, x] = att32[chunk, :].astype(jnp.bfloat16)
        at = attg.at[h, t, x]
        send(at, at, ("z", h), ("z1", h, 1), dp, along_z(1))
        send(at, at, ("z", h), ("z1", h, 3), dp, along_z(3))
        spread_x(h, 0)

    def tq(d):
        return ((zh + d) % 4) * 2 + c

    def xq(i):
        return (x + i) % 4

    lower, upper = slice(0, CH), slice(CH, CR)

    def hand(n, at):
        send(at, at, ("x", n), ("hand", n), dp, mate)

    def spread_x(n, d):
        at = attg.at[n, tq(d), x]
        send(at, at, ("x", n), ("x1", n, d, 1), along_x(1), t)
        send(at, at, ("x", n), ("x1", n, d, 3), along_x(3), t)
        hand(n, at)

    def z_first(n):
        received(("z1", n, 1), attg.at[n, tq(3), x])
        at = attg.at[n, tq(3), x, lower]
        send(at, at, ("z", n), ("z2", n), dp, along_z(1))
        received(("z1", n, 3), attg.at[n, tq(1), x])
        at = attg.at[n, tq(1), x, upper]
        send(at, at, ("z", n), ("z2", n), dp, along_z(3))
        spread_x(n, 3)
        spread_x(n, 1)

    def z_second(n):
        received(("z2", n), attg.at[n, tq(2), x])
        spread_x(n, 2)

    def x_first(n):
        for d in (0, 3, 1, 2):
            at = attg.at[n, tq(d), xq(3)]
            received(("x1", n, d, 1), at)
            send(at.at[lower], at.at[lower], ("x", n), ("x2", n), along_x(1), t)
            hand(n, at)
            at = attg.at[n, tq(d), xq(1)]
            received(("x1", n, d, 3), at)
            send(at.at[upper], at.at[upper], ("x", n), ("x2", n), along_x(3), t)
            hand(n, at)

    def x_second(n):
        received(("x2", n), attg.at[n, 0])
        for d in (0, 3, 1, 2):
            hand(n, attg.at[n, tq(d), xq(2)])

    def project(n):
        received(("hand", n), attg.at[n, 0:4])
        out = jnp.zeros((4 * CR, FEATURES), jnp.float32)
        for j in range(8):
            out += lax.dot_general(
                attg[n, j].reshape(4 * CR, QC),
                og[:, :, :, j * QC : (j + 1) * QC].reshape(FEATURES, QC),
                (((1,), (1,)), ((), ())),
                preferred_element_type=jnp.float32,
            )
        made[n] = out.astype(jnp.bfloat16).reshape(4, CR, FEATURES)
        for i in (2, 1, 3):
            send(made.at[n, xq(i)], gall.at[n, t, x], ("t", n), ("t", n), along_x(i), t)
        gall[n, t, x] = made[n, x]

    def gather_first(n):
        received(("t", n), made.at[n, 0:3])
        at = gall.at[n, t]
        send(at, at, ("u", n), ("u1", n, 1), dp, along_z(1))
        send(at, at, ("u", n), ("u1", n, 3), dp, along_z(3))
        send(at, at, ("u", n), ("last", n), dp, mate)

    def gather_second(n):
        for way in (1, 3):
            at = gall.at[n, tq(4 - way)]
            received(("u1", n, way), at)
            part = at.at[pl.ds(way - 1, 2)]
            send(part, part, ("u", n), ("u2", n), dp, along_z(way))
            send(at, at, ("u", n), ("last", n), dp, mate)

    def gather_third(n):
        at = gall.at[n, tq(2)]
        received(("u2", n), at)
        send(at, at, ("u", n), ("last", n), dp, mate)

    stores = []

    def store(src, dst):
        copy = pltpu.make_async_copy(src, dst, out_sem.at[len(stores)])
        copy.start()
        stores.append(copy)

    def finish(n):
        received(("last", n), gall.at[n, 0:4])
        for part in range(16):
            i, q, r = part // 4, (part // 2) % 2, part % 2
            for s in range(4):
                runs[part, :, s * 128 : (s + 1) * 128] = gall[
                    n, 4 * q + s, i, :, r * 128 : (r + 1) * 128
                ]
        ordered[...] = jnp.dot(
            runs[...].reshape(16 * CR, 512), turn[...], preferred_element_type=jnp.float32
        ).reshape(16, CR, 512)
        for m in range(CR // 16):
            rows = slice(n * CR + m * 16, n * CR + (m + 1) * 16)
            squares = jnp.zeros((16, 128), jnp.float32)
            for part in range(16):
                i, q, r = part // 4, (part // 2) % 2, part % 2
                for s in range(4):
                    at = (r * 16 + i * 4 + s) * 256 + q * 128
                    columns = slice(at, at + 128)
                    value = (
                        hidden[rows, columns].astype(jnp.float32)
                        + ordered[part, m * 16 : (m + 1) * 16, s * 128 : (s + 1) * 128]
                    )
                    new_v[rows, columns] = value.astype(jnp.bfloat16)
                    residual[:, columns] = value
                    squares += value * value
            mean_square = jnp.sum(squares, axis=-1, keepdims=True) * (1.0 / D)
            factor = lax.rsqrt(mean_square + epsilon)
            normed_v[rows, :] = (residual[...] * factor * post[...]).astype(jnp.bfloat16)
        rows = pl.ds(n * CR, CR)
        store(new_v.at[rows], new_out.at[rows])
        store(normed_v.at[rows], normed_out.at[rows])

    steps = []

    def at_time(when, name, act, *args):
        steps.append((when, len(steps), name, act, args))

    at_time(1.0, "cross0", cross, 0)
    at_time(2.0, "forward11", forward, 1, 1)
    at_time(3.0, "collect0", collect, 0)
    at_time(4.0, "att0", attend, 0)
    at_time(5.0, "att1", attend, 1)
    at_time(5.1, "forward10", forward, 1, 0)
    at_time(6.0, "cross1", cross, 1)
    at_time(7.5, "collect1", collect, 1)
    at_time(9.0, "att2", attend, 2)
    at_time(10.4, "att3", attend, 3)
    for n, when in enumerate((9.5, 11.0, 14.5, 16.0)):
        at_time(when, f"z_first{n}", z_first, n)
        at_time(when + 3.0, f"z_second{n}", z_second, n)
    for n, when in enumerate((15.0, 17.5, 21.0, 24.0)):
        at_time(when, f"x_first{n}", x_first, n)
        at_time(when + 3.2, f"x_second{n}", x_second, n)
    for n, when in enumerate((19.5, 22.5, 26.0, 30.0)):
        at_time(when, f"project{n}", project, n)
        at_time(when + 4.0, f"gather_first{n}", gather_first, n)
    for n, when in enumerate((28.0, 32.5, 37.0, 41.5)):
        at_time(when, f"gather_second{n}", gather_second, n)
        at_time(when + 3.0, f"gather_third{n}", gather_third, n)
        at_time(when + 5.0, f"finish{n}", finish, n)
    waited = False
    for when, _, name, act, args in sorted(steps, key=lambda step: step[:2]):
        if act is project and not waited:
            received("o2", og.at[:, 0:3])
            waited = True
        act(*args)

    store(fresh_v, fresh_out)
    store(value_v, value_out)
    departed("b1", wst.at[0:7])
    departed("a", a.at[0:7])
    departed("b", wg.at[0:3])
    departed("c", pst.at[:, :, 0:3])
    departed("z", zst)
    departed("o1", og.at[0, 0])
    departed("o2", og.at[:, 0:3])
    for n in range(CHUNKS):
        departed(("x", n), attg.at[n, 0:7])
        departed(("z", n), attg.at[n, 0, 0:3])
        departed(("t", n), made.at[n, 0:3])
        departed(("u", n), gall.at[n, 0:7])
    assert not in_size and not out_size
    for copy in stores:
        copy.wait()


def copy_out(a_in, b_in, c_in, d_in, a_out, b_out, c_out, d_out, a, b, c, d, sem):
    parts = 4
    rows = ROWS // parts
    ins, outs = [], []
    for src, hold, dst in ((a_in, a, a_out), (b_in, b, b_out)):
        for n in range(parts):
            at = pl.ds(n * rows, rows)
            ins.append((src.at[at], hold.at[at]))
            outs.append((hold.at[at], dst.at[at]))
    ins += [(c_in, c), (d_in, d)]
    outs += [(c, c_out), (d, d_out)]
    first = [pltpu.make_async_copy(s, h, sem.at[0, n]) for n, (s, h) in enumerate(ins)]
    second = [pltpu.make_async_copy(h, s, sem.at[1, n]) for n, (h, s) in enumerate(outs)]
    for copy in first:
        copy.start()
    for before, after in zip(first, second):
        before.wait()
        after.start()
    for copy in second:
        copy.wait()


def shards(
    hidden,
    q_weight,
    k_weight,
    v_weight,
    o_weight,
    input_gain,
    post_gain,
    key_cache,
    value_cache,
    lengths,
):
    kc = jnp.transpose(key_cache, (0, 2, 1, 3)).reshape(ROWS * CACHE, HEAD_DIM)
    vc = jnp.transpose(value_cache, (0, 2, 1, 3)).reshape(ROWS * CACHE, HEAD_DIM)
    bf16, f32 = jnp.bfloat16, jnp.float32
    dma = pltpu.SemaphoreType.DMA
    results = (
        jax.ShapeDtypeStruct((ROWS, D), bf16),
        jax.ShapeDtypeStruct((ROWS, D), bf16),
        jax.ShapeDtypeStruct((ROWS, HEAD_DIM), bf16),
        jax.ShapeDtypeStruct((ROWS, HEAD_DIM), bf16),
    )
    held = pl.pallas_call(
        kernel,
        out_shape=results,
        in_specs=[pl.BlockSpec(memory_space=pl.ANY)] * 10,
        out_specs=[pl.BlockSpec(memory_space=pl.ANY)] * 4,
        scratch_shapes=[
            pltpu.VMEM((ROWS, D), bf16),
            pltpu.VMEM((32, QD), f32),
            pltpu.VMEM((32, 1024), f32),
            pltpu.VMEM((32, 1024), f32),
            pltpu.VMEM((32, QD), f32),
            pltpu.VMEM((1, D), f32),
            pltpu.VMEM((1, D), f32),
            pltpu.VMEM((ROWS * CACHE, HEAD_DIM), bf16),
            pltpu.VMEM((ROWS * CACHE, HEAD_DIM), bf16),
            pltpu.VMEM((1, ROWS), jnp.int32),
            pltpu.VMEM((ROWS, 1), f32),
            pltpu.VMEM((ROWS, HEAD_DIM), f32),
            pltpu.VMEM((ROWS, HEAD_DIM), f32),
            pltpu.VMEM((8, ROWS, K), bf16),
            pltpu.VMEM((8, 32, WC), bf16),
            pltpu.VMEM((4, 8, 32, WC), bf16),
            pltpu.VMEM((2, 4, 32, QD), bf16),
            pltpu.VMEM((8, ROWS, K), bf16),
            pltpu.VMEM((2, 2, 4 * HALF, WC), f32),
            pltpu.VMEM((2, 2, 4, HALF, WC), bf16),
            pltpu.VMEM((2, 2, 2, QUARTER, WC), bf16),
            pltpu.VMEM((2, 2, 2, 2, QUARTER, WC), bf16),
            pltpu.VMEM((2, 2, 2, QUARTER, WC), bf16),
            pltpu.VMEM((2, HALF, WC), bf16),
            pltpu.VMEM((2, HALF, WC), bf16),
            pltpu.VMEM((ROWS, WC), f32),
            pltpu.VMEM((ROWS // BLOCK_ROWS, BLOCK_ROWS * GROUP, BLOCK_ROWS * CACHE), bf16),
            pltpu.VMEM((ROWS, QC), f32),
            pltpu.VMEM((CHUNKS, 8, 4, CR, QC), bf16),
            pltpu.VMEM((CHUNKS, 4, CR, FEATURES), bf16),
            pltpu.VMEM((CHUNKS, 8, 4, CR, FEATURES), bf16),
            pltpu.VMEM((512, 512), bf16),
            pltpu.VMEM((16, CR, 512), bf16),
            pltpu.VMEM((16, CR, 512), f32),
            pltpu.VMEM((16, D), f32),
            pltpu.VMEM((ROWS, D), bf16),
            pltpu.VMEM((ROWS, D), bf16),
            pltpu.VMEM((ROWS, HEAD_DIM), bf16),
            pltpu.VMEM((ROWS, HEAD_DIM), bf16),
            dma((10,)),
            dma((2 * CHUNKS + 2,)),
            dma((SENDS,)),
            dma((RECEIVES,)),
        ],
        compiler_params=pltpu.CompilerParams(collective_id=0, has_side_effects=True),
    )(
        hidden,
        q_weight,
        k_weight,
        v_weight,
        o_weight,
        input_gain.reshape(1, D),
        post_gain.reshape(1, D),
        kc,
        vc,
        lengths.reshape(1, ROWS),
    )
    new_hidden, normed, fresh, values = pl.pallas_call(
        copy_out,
        out_shape=results,
        in_specs=[pl.BlockSpec(memory_space=pl.ANY)] * 4,
        out_specs=[pl.BlockSpec(memory_space=pl.ANY)] * 4,
        scratch_shapes=[
            pltpu.VMEM((ROWS, D), bf16),
            pltpu.VMEM((ROWS, D), bf16),
            pltpu.VMEM((ROWS, HEAD_DIM), bf16),
            pltpu.VMEM((ROWS, HEAD_DIM), bf16),
            dma((2, 10)),
        ],
    )(*held)
    return (
        new_hidden,
        normed,
        fresh.reshape(ROWS, 1, HEAD_DIM),
        values.reshape(ROWS, 1, HEAD_DIM),
    )


def solution(mesh):
    in_specs = (
        P("dp", None),
        P(("dp", "tensor"), None),
        P(("dp", "tensor"), None),
        P(("dp", "tensor"), None),
        P(("dp", "tensor"), None),
        P(),
        P(),
        P("dp", None, "tensor", None),
        P("dp", None, "tensor", None),
        P("dp"),
    )
    out_specs = (P("dp", None), P("dp", None), P("dp", "tensor", None), P("dp", "tensor", None))
    return jax.shard_map(shards, mesh=mesh, in_specs=in_specs, out_specs=out_specs, check_vma=False)
```

time: 115 us -> 107 us (0.930)
  Pallas kernels: 114 us -> 106 us
    pallas_call x2, Pallas kernels: 114 us -> 106 us  [the longest x1 103 us: shards(): pl.pallas_call(kernel, out_shape=results, in_specs=[pl.BlockSpec(memory_s...]
where the time goes in v3:
time: 107 us
  Pallas kernels  106 us (99%)
    pallas_call x1, Pallas kernels, shards(): pl.pallas_call(kernel, out_shape=results, in_specs=[pl.BlockSpec(memory_s...  103 us
    pallas_call x1, Pallas kernels, shards(): pl.pallas_call(copy_out, out_shape=results, in_specs=[pl.BlockSpec(memory...  3.62 us

profile of v3, /device:TPU:1, one launch (start us, length us, event | category | flops | bytes accessed | tf_op | source)
XLA Modules:
  0.0 107.0 jit_solution(9861073714355901588)
XLA Ops:
  0.6 102.7 %shard_map.129 = (bf16[128,8192]{1,0:T(8,128)(2,1)}, bf16[128,8192]{1,0:T(8,128)(2,1)}, bf16[128,128]{1,0:T(8,128)(2,1)}, bf16[128,128]{1,0:T(8,128)(2,1)}) custom-call(bf16[128,8192]{1,0:T(8,128)(2,1)} %hidden_in.1, f32[32,4096]{1,0:T(8,128)} %qw_in.1, f32[32,1024]{1,0:T(8,128)} %kw_in.1, f32[32,1024]{1,0:T(8,128)} %vw_in.1, f32[32,4096]{1,0:T(8,128)} %ow_in.1, ...), custom_call_target="tpu_custom_call" | custom-call | tf_op jit(solution)/shard_map/pallas_call | solution.py:668
  103.3 3.6 %shard_map.130 = (bf16[128,8192]{1,0:T(8,128)(2,1)}, bf16[128,8192]{1,0:T(8,128)(2,1)}, bf16[128,128]{1,0:T(8,128)(2,1)}, bf16[128,128]{1,0:T(8,128)(2,1)}) custom-call(bf16[128,8192]{1,0:T(8,128)(2,1)} %get-tuple-element.12.a_in, bf16[128,8192]{1,0:T(8,128)(2,1)} %get-tuple-element.13.b_in, bf16[128,128]{1,0:T(8,128)(2,1)} %get-tuple-element.14.c_in, ...), custom_call_target="tpu_custom_call" | custom-call | tf_op jit(solution)/shard_map/pallas_call | solution.py:731
